TPU v7x, 256 devices: a whole 4x4x8 slice. The times are simulated.
256 devices in a mesh: section: 8 (over z_hi, x), dp: 32 (over z_lo, y, core).
Axes of the slice: x: 4, y: 4, z: 8 (z_hi: 2, z_lo: 4; z = z_hi * 4 + z_lo), core: 2. Of those that a mesh axis runs over, the one named last changes fastest.
Arguments:
- features: bfloat16 [1, 8, 4096, 4096], P(None, 'section', 'dp'), parts along dimension 2, may hold values from -6 to 6
- in_proj: bfloat16 [8, 4096, 512], P('section'), may hold values from -0.09375 to 0.09375
- mix_proj: bfloat16 [8, 2, 256, 256], P('section'), may hold values from -0.375 to 0.375
- out_proj: bfloat16 [8, 512, 4096], P('section'), may hold values from -0.375 to 0.375
- gate_proj: bfloat16 [8, 2, 4096], P('section'), may hold values from -0.09375 to 0.09375
- cross_bias: float32 [8, 4096], P('section'), may hold values from -3 to 3
Outputs:
- crossed: bfloat16 [1, 8, 4096, 4096], P(None, 'section', 'dp'), parts along dimension 2
There are 32 independent parts, one for each index of `dp`. A program takes and returns all parts, laid end to end along the dimension named above; an argument that names none is the same for every part. Nothing has to cross between parts.
All inputs are finite; a program needn't handle non-finite values.
Results may differ from a plain program's by a relative error of at most 0.015.
Values may be sent and summed in bfloat16 or wider, within the bound.
A program may use at most 64 MiB of HBM per device.

v0:
```python
import jax
import jax.numpy as jnp
from jax import lax
from jax.sharding import PartitionSpec as P


def from_behind(block, axis, distance):
    devices = range(lax.axis_size(axis))
    route = [(i - distance, i) for i in devices if i - distance in devices]
    return lax.ppermute(block, axis, route)


def cross_layer(current, anchor, v_mat, c_mat, u_mat, gate_mat, shift_row):
    row_count = current.shape[0]
    expert_count = c_mat.shape[0]
    rank_size = c_mat.shape[1]
    projected = jnp.dot(current, v_mat, preferred_element_type=jnp.float32)
    inner_first = (
        jnp.tanh(projected).astype(jnp.bfloat16).reshape(row_count, expert_count, rank_size)
    )
    inner_second = jnp.einsum(
        "rek,ekj->rej", inner_first, c_mat, preferred_element_type=jnp.float32
    )
    logits = lax.dot_general(
        current, gate_mat, (((1,), (1,)), ((), ())), preferred_element_type=jnp.float32
    )
    gate_values = 1.0 / jnp.sum(jnp.exp(logits[:, None, :] - logits[:, :, None]), axis=2)
    blended = (gate_values[:, :, None] * jnp.tanh(inner_second)).astype(jnp.bfloat16)
    blended = blended.reshape(row_count, expert_count * rank_size)
    crossed = jnp.dot(blended, u_mat, preferred_element_type=jnp.float32)
    updated = current.astype(jnp.float32) + anchor.astype(jnp.float32) * (crossed + shift_row)
    return updated.astype(jnp.bfloat16)


def per_device(features, in_proj, mix_proj, out_proj, gate_proj, cross_bias):
    section_count = lax.axis_size("section")
    position = lax.axis_index("section")
    pieces = 2
    local_micro = features.shape[0]
    row_count = features.shape[2]
    feature_count = features.shape[3]
    piece_rows = row_count // pieces
    everyone = lax.all_gather(features, "section", axis=1, tiled=True)
    all_units = everyone.reshape(local_micro * section_count * pieces, piece_rows, feature_count)
    unit_count = all_units.shape[0]
    step_count = unit_count + section_count - 1
    v_mat = in_proj[0]
    c_mat = mix_proj[0]
    u_mat = out_proj[0]
    gate_mat = gate_proj[0]
    shift_row = cross_bias[0]

    def apply_layer(current, anchor):
        return cross_layer(current, anchor, v_mat, c_mat, u_mat, gate_mat, shift_row)

    def keep_input(current, anchor):
        return current

    def advance(carried, moment):
        incoming, outgoing, collected = carried
        unit_here = moment - position
        active = (unit_here >= 0) & (unit_here < unit_count)
        anchor = lax.dynamic_index_in_dim(
            all_units, jnp.clip(unit_here, 0, unit_count - 1), 0, keepdims=False
        )
        current = jnp.where(position == 0, anchor, incoming)
        result = lax.cond(active, apply_layer, keep_input, current, anchor)
        outgoing = jnp.where(position == section_count - 1, result, outgoing)
        held_unit = moment + position - 2 * section_count + 2
        arrived = (
            (held_unit >= 0)
            & (held_unit < unit_count)
            & (held_unit // pieces % section_count == position)
        )
        held_safe = jnp.clip(held_unit, 0, unit_count - 1)
        slot_index = held_safe // pieces // section_count * pieces + held_safe % pieces
        previous = lax.dynamic_index_in_dim(collected, slot_index, 0, keepdims=False)
        collected = lax.dynamic_update_index_in_dim(
            collected, jnp.where(arrived, outgoing, previous), slot_index, 0
        )
        return (result, outgoing, collected)

    def forward_step(carried, moment):
        result, outgoing, collected = advance(carried, moment)
        incoming = from_behind(result, "section", 1)
        return ((incoming, outgoing, collected), None)

    def cycle_step(carried, moment):
        moved, _ = forward_step(carried, moment)
        incoming, outgoing, collected = moved
        outgoing = from_behind(outgoing, "section", -1)
        return ((incoming, outgoing, collected), None)

    blank = jnp.zeros((piece_rows, feature_count), jnp.bfloat16)
    holding = jnp.zeros((local_micro * pieces, piece_rows, feature_count), jnp.bfloat16)
    carried, _ = lax.scan(
        forward_step, (blank, blank, holding), jnp.arange(0, section_count - 1, dtype=jnp.int32)
    )
    carried, _ = lax.scan(
        cycle_step, carried, jnp.arange(section_count - 1, step_count - 1, dtype=jnp.int32)
    )
    _, _, collected = advance(carried, jnp.int32(step_count - 1))
    return collected.reshape(local_micro, 1, row_count, feature_count)


def solution(mesh):
    placed = (
        P(None, "section", "dp", None),
        P("section", None, None),
        P("section", None, None, None),
        P("section", None, None),
        P("section", None, None),
        P("section", None),
    )
    return jax.shard_map(
        per_device,
        mesh=mesh,
        in_specs=placed,
        out_specs=P(None, "section", "dp", None),
        check_vma=False,
    )
```

profile of v0, /device:TPU:160, one launch (start us, length us, event | category | flops | bytes accessed | tf_op | source)
XLA Modules:
  0.0 966.1 jit_solution(16218471225976274042)
XLA Ops:
  7.3 171.0 %all-gather.2.cloned.1.call-done = bf16[1,8,128,4096]{3,2,0,1:T(8,128)(2,1)} async-done(((bf16[1,1,128,4096]{3,2,0,1:T(8,128)(2,1)}), bf16[1,8,128,4096]{3,2,0,1:T(8,128)(2,1)}) %all-gather.2.cloned.1.call-update) | async-done | bytes 8388624 | tf_op jit(solution)/shard_map/all_gather | solution.py:43
  179.5 250.9 %while.40 = (s32[]{:T(128)}, bf16[64,4096]{1,0:T(8,128)(2,1)S(1)}, bf16[64,4096]{1,0:T(8,128)(2,1)S(1)}, bf16[2,64,4096]{2,1,0:T(8,128)(2,1)}, s32[7]{0:T(128)S(...) while((s32[]{:T(128)}, bf16[64,4096]{1,0:T(8,128)(2,1)S(1)}, ...), condition=%wide.region_4.5_spmd.clone, body=%wide.region_0.4_spmd.clone.sunk | while | flops 557416960 | bytes 37524112 | solution.py:96
  187.0 31.3 %collective-permute-done.2 = bf16[64,4096]{1,0:T(8,128)(2,1)S(1)} collective-permute-done((bf16[64,4096]{1,0:T(8,128)(2,1)S(1)}, bf16[64,4096]{1,0:T(8,128)(2,1)S(1)}, u32[]{:S(2)}, u32[]{:S(2)}) %collective-permute-start.2) | collective-permute-done | bytes 524320 | tf_op jit(solution)/shard_map/while/body/eval_jaxpr/ppermute | solution.py:10
  225.5 36.1 %collective-permute-done.2 = bf16[64,4096]{1,0:T(8,128)(2,1)S(1)} collective-permute-done((bf16[64,4096]{1,0:T(8,128)(2,1)S(1)}, bf16[64,4096]{1,0:T(8,128)(2,1)S(1)}, u32[]{:S(2)}, u32[]{:S(2)}) %collective-permute-start.2) | collective-permute-done | bytes 524320 | tf_op jit(solution)/shard_map/while/body/eval_jaxpr/ppermute | solution.py:10
  268.8 25.8 %collective-permute-done.2 = bf16[64,4096]{1,0:T(8,128)(2,1)S(1)} collective-permute-done((bf16[64,4096]{1,0:T(8,128)(2,1)S(1)}, bf16[64,4096]{1,0:T(8,128)(2,1)S(1)}, u32[]{:S(2)}, u32[]{:S(2)}) %collective-permute-start.2) | collective-permute-done | bytes 524320 | tf_op jit(solution)/shard_map/while/body/eval_jaxpr/ppermute | solution.py:10
  301.8 23.0 %collective-permute-done.2 = bf16[64,4096]{1,0:T(8,128)(2,1)S(1)} collective-permute-done((bf16[64,4096]{1,0:T(8,128)(2,1)S(1)}, bf16[64,4096]{1,0:T(8,128)(2,1)S(1)}, u32[]{:S(2)}, u32[]{:S(2)}) %collective-permute-start.2) | collective-permute-done | bytes 524320 | tf_op jit(solution)/shard_map/while/body/eval_jaxpr/ppermute | solution.py:10
  336.9 27.7 %collective-permute-done.2 = bf16[64,4096]{1,0:T(8,128)(2,1)S(1)} collective-permute-done((bf16[64,4096]{1,0:T(8,128)(2,1)S(1)}, bf16[64,4096]{1,0:T(8,128)(2,1)S(1)}, u32[]{:S(2)}, u32[]{:S(2)}) %collective-permute-start.2) | collective-permute-done | bytes 524320 | tf_op jit(solution)/shard_map/while/body/eval_jaxpr/ppermute | solution.py:10
  376.6 21.3 %collective-permute-done.2 = bf16[64,4096]{1,0:T(8,128)(2,1)S(1)} collective-permute-done((bf16[64,4096]{1,0:T(8,128)(2,1)S(1)}, bf16[64,4096]{1,0:T(8,128)(2,1)S(1)}, u32[]{:S(2)}, u32[]{:S(2)}) %collective-permute-start.2) | collective-permute-done | bytes 524320 | tf_op jit(solution)/shard_map/while/body/eval_jaxpr/ppermute | solution.py:10
  409.9 20.4 %collective-permute-done.2 = bf16[64,4096]{1,0:T(8,128)(2,1)S(1)} collective-permute-done((bf16[64,4096]{1,0:T(8,128)(2,1)S(1)}, bf16[64,4096]{1,0:T(8,128)(2,1)S(1)}, u32[]{:S(2)}, u32[]{:S(2)}) %collective-permute-start.2) | collective-permute-done | bytes 524320 | tf_op jit(solution)/shard_map/while/body/eval_jaxpr/ppermute | solution.py:10
  430.3 525.7 %while.39 = (s32[]{:T(128)}, bf16[64,4096]{1,0:T(8,128)(2,1)S(1)}, bf16[64,4096]{1,0:T(8,128)(2,1)S(1)}, bf16[2,64,4096]{2,1,0:T(8,128)(2,1)}, s32[15]{0:T(128)S...) while((s32[]{:T(128)}, bf16[64,4096]{1,0:T(8,128)(2,1)S(1)}, ...), condition=%wide.region_9.10_spmd, body=%wide.region_5.9_spmd.sunk | while | flops 557154816 | bytes 39621292 | solution.py:99
  446.2 12.7 %collective-permute-done.1 = bf16[64,4096]{1,0:T(8,128)(2,1)S(1)} collective-permute-done((bf16[64,4096]{1,0:T(8,128)(2,1)S(1)}, bf16[64,4096]{1,0:T(8,128)(2,1)S(1)}, u32[]{:S(2)}, u32[]{:S(2)}) %collective-permute-start.1) | collective-permute-done | bytes 524320 | tf_op jit(solution)/shard_map/while/body/eval_jaxpr/ppermute | solution.py:10
  459.0 10.1 %collective-permute-done = bf16[64,4096]{1,0:T(8,128)(2,1)S(1)} collective-permute-done((bf16[64,4096]{1,0:T(8,128)(2,1)S(1)}, bf16[64,4096]{1,0:T(8,128)(2,1)S(1)}, u32[]{:S(2)}, u32[]{:S(2)}) %collective-permute-start) | collective-permute-done | bytes 524320 | tf_op jit(solution)/shard_map/while/body/eval_jaxpr/ppermute | solution.py:10
  485.0 13.6 %collective-permute-done.1 = bf16[64,4096]{1,0:T(8,128)(2,1)S(1)} collective-permute-done((bf16[64,4096]{1,0:T(8,128)(2,1)S(1)}, bf16[64,4096]{1,0:T(8,128)(2,1)S(1)}, u32[]{:S(2)}, u32[]{:S(2)}) %collective-permute-start.1) | collective-permute-done | bytes 524320 | tf_op jit(solution)/shard_map/while/body/eval_jaxpr/ppermute | solution.py:10
  498.6 10.1 %collective-permute-done = bf16[64,4096]{1,0:T(8,128)(2,1)S(1)} collective-permute-done((bf16[64,4096]{1,0:T(8,128)(2,1)S(1)}, bf16[64,4096]{1,0:T(8,128)(2,1)S(1)}, u32[]{:S(2)}, u32[]{:S(2)}) %collective-permute-start) | collective-permute-done | bytes 524320 | tf_op jit(solution)/shard_map/while/body/eval_jaxpr/ppermute | solution.py:10
  524.6 17.9 %collective-permute-done.1 = bf16[64,4096]{1,0:T(8,128)(2,1)S(1)} collective-permute-done((bf16[64,4096]{1,0:T(8,128)(2,1)S(1)}, bf16[64,4096]{1,0:T(8,128)(2,1)S(1)}, u32[]{:S(2)}, u32[]{:S(2)}) %collective-permute-start.1) | collective-permute-done | bytes 524320 | tf_op jit(solution)/shard_map/while/body/eval_jaxpr/ppermute | solution.py:10
  542.5 10.4 %collective-permute-done = bf16[64,4096]{1,0:T(8,128)(2,1)S(1)} collective-permute-done((bf16[64,4096]{1,0:T(8,128)(2,1)S(1)}, bf16[64,4096]{1,0:T(8,128)(2,1)S(1)}, u32[]{:S(2)}, u32[]{:S(2)}) %collective-permute-start) | collective-permute-done | bytes 524320 | tf_op jit(solution)/shard_map/while/body/eval_jaxpr/ppermute | solution.py:10
  568.8 9.9 %collective-permute-done.1 = bf16[64,4096]{1,0:T(8,128)(2,1)S(1)} collective-permute-done((bf16[64,4096]{1,0:T(8,128)(2,1)S(1)}, bf16[64,4096]{1,0:T(8,128)(2,1)S(1)}, u32[]{:S(2)}, u32[]{:S(2)}) %collective-permute-start.1) | collective-permute-done | bytes 524320 | tf_op jit(solution)/shard_map/while/body/eval_jaxpr/ppermute | solution.py:10
  578.7 8.3 collective-permute-done
  602.9 12.8 %collective-permute-done.1 = bf16[64,4096]{1,0:T(8,128)(2,1)S(1)} collective-permute-done((bf16[64,4096]{1,0:T(8,128)(2,1)S(1)}, bf16[64,4096]{1,0:T(8,128)(2,1)S(1)}, u32[]{:S(2)}, u32[]{:S(2)}) %collective-permute-start.1) | collective-permute-done | bytes 524320 | tf_op jit(solution)/shard_map/while/body/eval_jaxpr/ppermute | solution.py:10
  615.7 10.1 %collective-permute-done = bf16[64,4096]{1,0:T(8,128)(2,1)S(1)} collective-permute-done((bf16[64,4096]{1,0:T(8,128)(2,1)S(1)}, bf16[64,4096]{1,0:T(8,128)(2,1)S(1)}, u32[]{:S(2)}, u32[]{:S(2)}) %collective-permute-start) | collective-permute-done | bytes 524320 | tf_op jit(solution)/shard_map/while/body/eval_jaxpr/ppermute | solution.py:10
  641.8 17.2 %collective-permute-done.1 = bf16[64,4096]{1,0:T(8,128)(2,1)S(1)} collective-permute-done((bf16[64,4096]{1,0:T(8,128)(2,1)S(1)}, bf16[64,4096]{1,0:T(8,128)(2,1)S(1)}, u32[]{:S(2)}, u32[]{:S(2)}) %collective-permute-start.1) | collective-permute-done | bytes 524320 | tf_op jit(solution)/shard_map/while/body/eval_jaxpr/ppermute | solution.py:10
  658.9 10.4 %collective-permute-done = bf16[64,4096]{1,0:T(8,128)(2,1)S(1)} collective-permute-done((bf16[64,4096]{1,0:T(8,128)(2,1)S(1)}, bf16[64,4096]{1,0:T(8,128)(2,1)S(1)}, u32[]{:S(2)}, u32[]{:S(2)}) %collective-permute-start) | collective-permute-done | bytes 524320 | tf_op jit(solution)/shard_map/while/body/eval_jaxpr/ppermute | solution.py:10
  685.2 9.9 %collective-permute-done.1 = bf16[64,4096]{1,0:T(8,128)(2,1)S(1)} collective-permute-done((bf16[64,4096]{1,0:T(8,128)(2,1)S(1)}, bf16[64,4096]{1,0:T(8,128)(2,1)S(1)}, u32[]{:S(2)}, u32[]{:S(2)}) %collective-permute-start.1) | collective-permute-done | bytes 524320 | tf_op jit(solution)/shard_map/while/body/eval_jaxpr/ppermute | solution.py:10
  695.1 7.9 collective-permute-done
  719.0 18.1 %collective-permute-done.1 = bf16[64,4096]{1,0:T(8,128)(2,1)S(1)} collective-permute-done((bf16[64,4096]{1,0:T(8,128)(2,1)S(1)}, bf16[64,4096]{1,0:T(8,128)(2,1)S(1)}, u32[]{:S(2)}, u32[]{:S(2)}) %collective-permute-start.1) | collective-permute-done | bytes 524320 | tf_op jit(solution)/shard_map/while/body/eval_jaxpr/ppermute | solution.py:10
  737.0 10.1 %collective-permute-done = bf16[64,4096]{1,0:T(8,128)(2,1)S(1)} collective-permute-done((bf16[64,4096]{1,0:T(8,128)(2,1)S(1)}, bf16[64,4096]{1,0:T(8,128)(2,1)S(1)}, u32[]{:S(2)}, u32[]{:S(2)}) %collective-permute-start) | collective-permute-done | bytes 524320 | tf_op jit(solution)/shard_map/while/body/eval_jaxpr/ppermute | solution.py:10
  770.5 10.4 %collective-permute-done = bf16[64,4096]{1,0:T(8,128)(2,1)S(1)} collective-permute-done((bf16[64,4096]{1,0:T(8,128)(2,1)S(1)}, bf16[64,4096]{1,0:T(8,128)(2,1)S(1)}, u32[]{:S(2)}, u32[]{:S(2)}) %collective-permute-start) | collective-permute-done | bytes 524320 | tf_op jit(solution)/shard_map/while/body/eval_jaxpr/ppermute | solution.py:10
  796.8 9.0 collective-permute-done.1
  805.8 7.9 collective-permute-done
  829.6 8.2 collective-permute-done.1
  837.8 7.9 collective-permute-done
  868.9 7.9 collective-permute-done
  (406 shorter events, 399.0 us)
Async XLA Ops:
  6.5 171.8 %all-gather.2.cloned.1.call-start = ((), (), s32[]{:S(2)}) async-start(), calls=%async_computation | async-start | bytes 9437184 | tf_op jit(solution)/shard_map/all_gather | solution.py:43
  181.9 36.4 %collective-permute-start.2 = (bf16[64,4096]{1,0:T(8,128)(2,1)S(1)}, bf16[64,4096]{1,0:T(8,128)(2,1)S(1)}, u32[]{:S(2)}, u32[]{:S(2)}) collective-permute-start(bf16[64,4096]{1,0:T(8,128)(2,1)S(1)} %get-tuple-element.1181), channel_id=1, source_target_pairs={{0,32},{32,64},{64,96},{96,128},{128,160},{160,192},{192,224},{1,3... | collective-permute-start | bytes 1572872 | tf_op jit(solution)/shard_map/while/body/eval_jaxpr/ppermute | solution.py:10
  220.7 40.9 %collective-permute-start.2 = (bf16[64,4096]{1,0:T(8,128)(2,1)S(1)}, bf16[64,4096]{1,0:T(8,128)(2,1)S(1)}, u32[]{:S(2)}, u32[]{:S(2)}) collective-permute-start(bf16[64,4096]{1,0:T(8,128)(2,1)S(1)} %get-tuple-element.1181), channel_id=1, source_target_pairs={{0,32},{32,64},{64,96},{96,128},{128,160},{160,192},{192,224},{1,3... | collective-permute-start | bytes 1572872 | tf_op jit(solution)/shard_map/while/body/eval_jaxpr/ppermute | solution.py:10
  264.0 30.6 %collective-permute-start.2 = (bf16[64,4096]{1,0:T(8,128)(2,1)S(1)}, bf16[64,4096]{1,0:T(8,128)(2,1)S(1)}, u32[]{:S(2)}, u32[]{:S(2)}) collective-permute-start(bf16[64,4096]{1,0:T(8,128)(2,1)S(1)} %get-tuple-element.1181), channel_id=1, source_target_pairs={{0,32},{32,64},{64,96},{96,128},{128,160},{160,192},{192,224},{1,3... | collective-permute-start | bytes 1572872 | tf_op jit(solution)/shard_map/while/body/eval_jaxpr/ppermute | solution.py:10
  297.0 27.8 %collective-permute-start.2 = (bf16[64,4096]{1,0:T(8,128)(2,1)S(1)}, bf16[64,4096]{1,0:T(8,128)(2,1)S(1)}, u32[]{:S(2)}, u32[]{:S(2)}) collective-permute-start(bf16[64,4096]{1,0:T(8,128)(2,1)S(1)} %get-tuple-element.1181), channel_id=1, source_target_pairs={{0,32},{32,64},{64,96},{96,128},{128,160},{160,192},{192,224},{1,3... | collective-permute-start | bytes 1572872 | tf_op jit(solution)/shard_map/while/body/eval_jaxpr/ppermute | solution.py:10
  332.0 32.6 %collective-permute-start.2 = (bf16[64,4096]{1,0:T(8,128)(2,1)S(1)}, bf16[64,4096]{1,0:T(8,128)(2,1)S(1)}, u32[]{:S(2)}, u32[]{:S(2)}) collective-permute-start(bf16[64,4096]{1,0:T(8,128)(2,1)S(1)} %get-tuple-element.1181), channel_id=1, source_target_pairs={{0,32},{32,64},{64,96},{96,128},{128,160},{160,192},{192,224},{1,3... | collective-permute-start | bytes 1572872 | tf_op jit(solution)/shard_map/while/body/eval_jaxpr/ppermute | solution.py:10
  371.8 26.1 %collective-permute-start.2 = (bf16[64,4096]{1,0:T(8,128)(2,1)S(1)}, bf16[64,4096]{1,0:T(8,128)(2,1)S(1)}, u32[]{:S(2)}, u32[]{:S(2)}) collective-permute-start(bf16[64,4096]{1,0:T(8,128)(2,1)S(1)} %get-tuple-element.1181), channel_id=1, source_target_pairs={{0,32},{32,64},{64,96},{96,128},{128,160},{160,192},{192,224},{1,3... | collective-permute-start | bytes 1572872 | tf_op jit(solution)/shard_map/while/body/eval_jaxpr/ppermute | solution.py:10
  405.1 25.3 %collective-permute-start.2 = (bf16[64,4096]{1,0:T(8,128)(2,1)S(1)}, bf16[64,4096]{1,0:T(8,128)(2,1)S(1)}, u32[]{:S(2)}, u32[]{:S(2)}) collective-permute-start(bf16[64,4096]{1,0:T(8,128)(2,1)S(1)} %get-tuple-element.1181), channel_id=1, source_target_pairs={{0,32},{32,64},{64,96},{96,128},{128,160},{160,192},{192,224},{1,3... | collective-permute-start | bytes 1572872 | tf_op jit(solution)/shard_map/while/body/eval_jaxpr/ppermute | solution.py:10
  440.4 18.6 %collective-permute-start.1 = (bf16[64,4096]{1,0:T(8,128)(2,1)S(1)}, bf16[64,4096]{1,0:T(8,128)(2,1)S(1)}, u32[]{:S(2)}, u32[]{:S(2)}) collective-permute-start(bf16[64,4096]{1,0:T(8,128)(2,1)S(1)} %get-tuple-element.1015), channel_id=1, source_target_pairs={{32,0},{64,32},{96,64},{128,96},{160,128},{192,160},{224,192},{33,... | collective-permute-start | bytes 1572872 | tf_op jit(solution)/shard_map/while/body/eval_jaxpr/ppermute | solution.py:10
  442.3 26.8 %collective-permute-start = (bf16[64,4096]{1,0:T(8,128)(2,1)S(1)}, bf16[64,4096]{1,0:T(8,128)(2,1)S(1)}, u32[]{:S(2)}, u32[]{:S(2)}) collective-permute-start(bf16[64,4096]{1,0:T(8,128)(2,1)S(1)} %get-tuple-element.1180), channel_id=1, source_target_pairs={{0,32},{32,64},{64,96},{96,128},{128,160},{160,192},{192,224},{1,3... | collective-permute-start | bytes 1572872 | tf_op jit(solution)/shard_map/while/body/eval_jaxpr/ppermute | solution.py:10
  479.2 19.4 %collective-permute-start.1 = (bf16[64,4096]{1,0:T(8,128)(2,1)S(1)}, bf16[64,4096]{1,0:T(8,128)(2,1)S(1)}, u32[]{:S(2)}, u32[]{:S(2)}) collective-permute-start(bf16[64,4096]{1,0:T(8,128)(2,1)S(1)} %get-tuple-element.1015), channel_id=1, source_target_pairs={{32,0},{64,32},{96,64},{128,96},{160,128},{192,160},{224,192},{33,... | collective-permute-start | bytes 1572872 | tf_op jit(solution)/shard_map/while/body/eval_jaxpr/ppermute | solution.py:10
  481.1 27.6 %collective-permute-start = (bf16[64,4096]{1,0:T(8,128)(2,1)S(1)}, bf16[64,4096]{1,0:T(8,128)(2,1)S(1)}, u32[]{:S(2)}, u32[]{:S(2)}) collective-permute-start(bf16[64,4096]{1,0:T(8,128)(2,1)S(1)} %get-tuple-element.1180), channel_id=1, source_target_pairs={{0,32},{32,64},{64,96},{96,128},{128,160},{160,192},{192,224},{1,3... | collective-permute-start | bytes 1572872 | tf_op jit(solution)/shard_map/while/body/eval_jaxpr/ppermute | solution.py:10
  518.8 23.8 %collective-permute-start.1 = (bf16[64,4096]{1,0:T(8,128)(2,1)S(1)}, bf16[64,4096]{1,0:T(8,128)(2,1)S(1)}, u32[]{:S(2)}, u32[]{:S(2)}) collective-permute-start(bf16[64,4096]{1,0:T(8,128)(2,1)S(1)} %get-tuple-element.1015), channel_id=1, source_target_pairs={{32,0},{64,32},{96,64},{128,96},{160,128},{192,160},{224,192},{33,... | collective-permute-start | bytes 1572872 | tf_op jit(solution)/shard_map/while/body/eval_jaxpr/ppermute | solution.py:10
  520.7 32.2 %collective-permute-start = (bf16[64,4096]{1,0:T(8,128)(2,1)S(1)}, bf16[64,4096]{1,0:T(8,128)(2,1)S(1)}, u32[]{:S(2)}, u32[]{:S(2)}) collective-permute-start(bf16[64,4096]{1,0:T(8,128)(2,1)S(1)} %get-tuple-element.1180), channel_id=1, source_target_pairs={{0,32},{32,64},{64,96},{96,128},{128,160},{160,192},{192,224},{1,3... | collective-permute-start | bytes 1572872 | tf_op jit(solution)/shard_map/while/body/eval_jaxpr/ppermute | solution.py:10
  563.0 15.7 %collective-permute-start.1 = (bf16[64,4096]{1,0:T(8,128)(2,1)S(1)}, bf16[64,4096]{1,0:T(8,128)(2,1)S(1)}, u32[]{:S(2)}, u32[]{:S(2)}) collective-permute-start(bf16[64,4096]{1,0:T(8,128)(2,1)S(1)} %get-tuple-element.1015), channel_id=1, source_target_pairs={{32,0},{64,32},{96,64},{128,96},{160,128},{192,160},{224,192},{33,... | collective-permute-start | bytes 1572872 | tf_op jit(solution)/shard_map/while/body/eval_jaxpr/ppermute | solution.py:10
  564.9 22.1 %collective-permute-start = (bf16[64,4096]{1,0:T(8,128)(2,1)S(1)}, bf16[64,4096]{1,0:T(8,128)(2,1)S(1)}, u32[]{:S(2)}, u32[]{:S(2)}) collective-permute-start(bf16[64,4096]{1,0:T(8,128)(2,1)S(1)} %get-tuple-element.1180), channel_id=1, source_target_pairs={{0,32},{32,64},{64,96},{96,128},{128,160},{160,192},{192,224},{1,3... | collective-permute-start | bytes 1572872 | tf_op jit(solution)/shard_map/while/body/eval_jaxpr/ppermute | solution.py:10
  597.1 18.7 %collective-permute-start.1 = (bf16[64,4096]{1,0:T(8,128)(2,1)S(1)}, bf16[64,4096]{1,0:T(8,128)(2,1)S(1)}, u32[]{:S(2)}, u32[]{:S(2)}) collective-permute-start(bf16[64,4096]{1,0:T(8,128)(2,1)S(1)} %get-tuple-element.1015), channel_id=1, source_target_pairs={{32,0},{64,32},{96,64},{128,96},{160,128},{192,160},{224,192},{33,... | collective-permute-start | bytes 1572872 | tf_op jit(solution)/shard_map/while/body/eval_jaxpr/ppermute | solution.py:10
  599.0 26.9 %collective-permute-start = (bf16[64,4096]{1,0:T(8,128)(2,1)S(1)}, bf16[64,4096]{1,0:T(8,128)(2,1)S(1)}, u32[]{:S(2)}, u32[]{:S(2)}) collective-permute-start(bf16[64,4096]{1,0:T(8,128)(2,1)S(1)} %get-tuple-element.1180), channel_id=1, source_target_pairs={{0,32},{32,64},{64,96},{96,128},{128,160},{160,192},{192,224},{1,3... | collective-permute-start | bytes 1572872 | tf_op jit(solution)/shard_map/while/body/eval_jaxpr/ppermute | solution.py:10
  635.9 23.0 %collective-permute-start.1 = (bf16[64,4096]{1,0:T(8,128)(2,1)S(1)}, bf16[64,4096]{1,0:T(8,128)(2,1)S(1)}, u32[]{:S(2)}, u32[]{:S(2)}) collective-permute-start(bf16[64,4096]{1,0:T(8,128)(2,1)S(1)} %get-tuple-element.1015), channel_id=1, source_target_pairs={{32,0},{64,32},{96,64},{128,96},{160,128},{192,160},{224,192},{33,... | collective-permute-start | bytes 1572872 | tf_op jit(solution)/shard_map/while/body/eval_jaxpr/ppermute | solution.py:10
  637.8 31.5 %collective-permute-start = (bf16[64,4096]{1,0:T(8,128)(2,1)S(1)}, bf16[64,4096]{1,0:T(8,128)(2,1)S(1)}, u32[]{:S(2)}, u32[]{:S(2)}) collective-permute-start(bf16[64,4096]{1,0:T(8,128)(2,1)S(1)} %get-tuple-element.1180), channel_id=1, source_target_pairs={{0,32},{32,64},{64,96},{96,128},{128,160},{160,192},{192,224},{1,3... | collective-permute-start | bytes 1572872 | tf_op jit(solution)/shard_map/while/body/eval_jaxpr/ppermute | solution.py:10
  679.4 15.7 %collective-permute-start.1 = (bf16[64,4096]{1,0:T(8,128)(2,1)S(1)}, bf16[64,4096]{1,0:T(8,128)(2,1)S(1)}, u32[]{:S(2)}, u32[]{:S(2)}) collective-permute-start(bf16[64,4096]{1,0:T(8,128)(2,1)S(1)} %get-tuple-element.1015), channel_id=1, source_target_pairs={{32,0},{64,32},{96,64},{128,96},{160,128},{192,160},{224,192},{33,... | collective-permute-start | bytes 1572872 | tf_op jit(solution)/shard_map/while/body/eval_jaxpr/ppermute | solution.py:10
  681.3 21.8 %collective-permute-start = (bf16[64,4096]{1,0:T(8,128)(2,1)S(1)}, bf16[64,4096]{1,0:T(8,128)(2,1)S(1)}, u32[]{:S(2)}, u32[]{:S(2)}) collective-permute-start(bf16[64,4096]{1,0:T(8,128)(2,1)S(1)} %get-tuple-element.1180), channel_id=1, source_target_pairs={{0,32},{32,64},{64,96},{96,128},{128,160},{160,192},{192,224},{1,3... | collective-permute-start | bytes 1572872 | tf_op jit(solution)/shard_map/while/body/eval_jaxpr/ppermute | solution.py:10
  713.1 23.9 %collective-permute-start.1 = (bf16[64,4096]{1,0:T(8,128)(2,1)S(1)}, bf16[64,4096]{1,0:T(8,128)(2,1)S(1)}, u32[]{:S(2)}, u32[]{:S(2)}) collective-permute-start(bf16[64,4096]{1,0:T(8,128)(2,1)S(1)} %get-tuple-element.1015), channel_id=1, source_target_pairs={{32,0},{64,32},{96,64},{128,96},{160,128},{192,160},{224,192},{33,... | collective-permute-start | bytes 1572872 | tf_op jit(solution)/shard_map/while/body/eval_jaxpr/ppermute | solution.py:10
  715.0 32.1 %collective-permute-start = (bf16[64,4096]{1,0:T(8,128)(2,1)S(1)}, bf16[64,4096]{1,0:T(8,128)(2,1)S(1)}, u32[]{:S(2)}, u32[]{:S(2)}) collective-permute-start(bf16[64,4096]{1,0:T(8,128)(2,1)S(1)} %get-tuple-element.1180), channel_id=1, source_target_pairs={{0,32},{32,64},{64,96},{96,128},{128,160},{160,192},{192,224},{1,3... | collective-permute-start | bytes 1572872 | tf_op jit(solution)/shard_map/while/body/eval_jaxpr/ppermute | solution.py:10
  759.1 21.8 %collective-permute-start = (bf16[64,4096]{1,0:T(8,128)(2,1)S(1)}, bf16[64,4096]{1,0:T(8,128)(2,1)S(1)}, u32[]{:S(2)}, u32[]{:S(2)}) collective-permute-start(bf16[64,4096]{1,0:T(8,128)(2,1)S(1)} %get-tuple-element.1180), channel_id=1, source_target_pairs={{0,32},{32,64},{64,96},{96,128},{128,160},{160,192},{192,224},{1,3... | collective-permute-start | bytes 1572872 | tf_op jit(solution)/shard_map/while/body/eval_jaxpr/ppermute | solution.py:10
  790.9 14.9 %collective-permute-start.1 = (bf16[64,4096]{1,0:T(8,128)(2,1)S(1)}, bf16[64,4096]{1,0:T(8,128)(2,1)S(1)}, u32[]{:S(2)}, u32[]{:S(2)}) collective-permute-start(bf16[64,4096]{1,0:T(8,128)(2,1)S(1)} %get-tuple-element.1015), channel_id=1, source_target_pairs={{32,0},{64,32},{96,64},{128,96},{160,128},{192,160},{224,192},{33,... | collective-permute-start | bytes 1572872 | tf_op jit(solution)/shard_map/while/body/eval_jaxpr/ppermute | solution.py:10
  792.8 20.9 %collective-permute-start = (bf16[64,4096]{1,0:T(8,128)(2,1)S(1)}, bf16[64,4096]{1,0:T(8,128)(2,1)S(1)}, u32[]{:S(2)}, u32[]{:S(2)}) collective-permute-start(bf16[64,4096]{1,0:T(8,128)(2,1)S(1)} %get-tuple-element.1180), channel_id=1, source_target_pairs={{0,32},{32,64},{64,96},{96,128},{128,160},{160,192},{192,224},{1,3... | collective-permute-start | bytes 1572872 | tf_op jit(solution)/shard_map/while/body/eval_jaxpr/ppermute | solution.py:10
  825.7 20.0 %collective-permute-start = (bf16[64,4096]{1,0:T(8,128)(2,1)S(1)}, bf16[64,4096]{1,0:T(8,128)(2,1)S(1)}, u32[]{:S(2)}, u32[]{:S(2)}) collective-permute-start(bf16[64,4096]{1,0:T(8,128)(2,1)S(1)} %get-tuple-element.1180), channel_id=1, source_target_pairs={{0,32},{32,64},{64,96},{96,128},{128,160},{160,192},{192,224},{1,3... | collective-permute-start | bytes 1572872 | tf_op jit(solution)/shard_map/while/body/eval_jaxpr/ppermute | solution.py:10
  857.7 19.2 %collective-permute-start = (bf16[64,4096]{1,0:T(8,128)(2,1)S(1)}, bf16[64,4096]{1,0:T(8,128)(2,1)S(1)}, u32[]{:S(2)}, u32[]{:S(2)}) collective-permute-start(bf16[64,4096]{1,0:T(8,128)(2,1)S(1)} %get-tuple-element.1180), channel_id=1, source_target_pairs={{0,32},{32,64},{64,96},{96,128},{128,160},{160,192},{192,224},{1,3... | collective-permute-start | bytes 1572872 | tf_op jit(solution)/shard_map/while/body/eval_jaxpr/ppermute | solution.py:10
  888.9 18.3 %collective-permute-start = (bf16[64,4096]{1,0:T(8,128)(2,1)S(1)}, bf16[64,4096]{1,0:T(8,128)(2,1)S(1)}, u32[]{:S(2)}, u32[]{:S(2)}) collective-permute-start(bf16[64,4096]{1,0:T(8,128)(2,1)S(1)} %get-tuple-element.1180), channel_id=1, source_target_pairs={{0,32},{32,64},{64,96},{96,128},{128,160},{160,192},{192,224},{1,3... | collective-permute-start | bytes 1572872 | tf_op jit(solution)/shard_map/while/body/eval_jaxpr/ppermute | solution.py:10
  914.4 17.5 %collective-permute-start = (bf16[64,4096]{1,0:T(8,128)(2,1)S(1)}, bf16[64,4096]{1,0:T(8,128)(2,1)S(1)}, u32[]{:S(2)}, u32[]{:S(2)}) collective-permute-start(bf16[64,4096]{1,0:T(8,128)(2,1)S(1)} %get-tuple-element.1180), channel_id=1, source_target_pairs={{0,32},{32,64},{64,96},{96,128},{128,160},{160,192},{192,224},{1,3... | collective-permute-start | bytes 1572872 | tf_op jit(solution)/shard_map/while/body/eval_jaxpr/ppermute | solution.py:10
  939.0 17.1 %collective-permute-start = (bf16[64,4096]{1,0:T(8,128)(2,1)S(1)}, bf16[64,4096]{1,0:T(8,128)(2,1)S(1)}, u32[]{:S(2)}, u32[]{:S(2)}) collective-permute-start(bf16[64,4096]{1,0:T(8,128)(2,1)S(1)} %get-tuple-element.1180), channel_id=1, source_target_pairs={{0,32},{32,64},{64,96},{96,128},{128,160},{160,192},{192,224},{1,3... | collective-permute-start | bytes 1572872 | tf_op jit(solution)/shard_map/while/body/eval_jaxpr/ppermute | solution.py:10
  (70 other events, 303.2 us)
Sparse Core Ops, SparseCore 0:
  10.0 168.3 all-gather.1
where the time goes:
time: 970 us; the launch traced here: 966 us
  waiting for transfers between devices  654 us (67%)
  starting transfers between devices  101 us (10%)
  matrix products  73.6 us (8%)
  other arithmetic  50.4 us (5%)
  local copies, waits for them, and re-layouts  40.5 us (4%)
  loops' own time  32.8 us (3%)
  between operations  13.5 us (1%)
    ppermute x37, waiting for transfers between devices, from_behind(): return lax.ppermute(block, axis, route)  482 us
    all_gather x1, waiting for transfers between devices, per_device(): everyone = lax.all_gather(features, 'section', axis=1, tiled=True)  171 us
    ppermute x37, starting transfers between devices, from_behind(): return lax.ppermute(block, axis, route)  101 us
    dot_general x16, matrix products, cross_layer(): projected = jnp.dot(current, v_mat, preferred_element_type=jnp.float32)  51 us
    select_n x23, other arithmetic, advance(): current = jnp.where(position == 0, anchor, incoming)  25.7 us
    dynamic_slice x23, local copies, waits for them, and re-layouts, advance(): lax.dynamic_index_in_dim(collected, slot_index, 0, keepdims=False)  24.9 us
    dynamic_update_slice x23, other arithmetic, advance(): lax.dynamic_update_index_in_dim(collected, jnp.where(arrived, outgoing, p...  24 us
    another operation x1, loops' own time, per_device(): lax.scan(cycle_step, carried, jnp.arange(section_count - 1, step_count -...  21 us
  transfers between devices with their start and end apart: 38, of which 38 were waited for; matrix products, arithmetic and copies ran while one was open for 2% of the time, Pallas kernels for 0%

commit v1 on v0

v1 whole, which is shorter than its diff:
```python
import functools
import random

import jax
import jax.numpy as jnp
from jax import lax
from jax.experimental import pallas as pl
from jax.experimental.pallas import tpu as pltpu
from jax.sharding import PartitionSpec as P

MESH = pl.DeviceIdType.MESH
NX, NH, NK, NY, NQ = 4, 2, 4, 4, 2
NZ = NH * NK
LAYERS = NX * NH
CHUNKS = 17
LINKS = 5
LAG = 2
SLOTS = 4
NONE = 255
ORDER_WEIGHT, RARE_WEIGHT, NOISE, SEED = 0.6, 3.0, 0.5, 0


def plan_routes():
    rnd = random.Random(SEED)
    nodes = [(x, z, q) for x in range(NX) for z in range(NZ) for q in range(NQ)]
    index = {n: i for i, n in enumerate(nodes)}
    count = len(nodes)
    goes = []
    for x, z, q in nodes:
        goes.append([
            index[((x + 1) % NX, z, q)], index[((x - 1) % NX, z, q)],
            index[(x, (z + 1) % NZ, q)], index[(x, (z - 1) % NZ, q)], index[(x, z, 1 - q)],
        ])
    held = [{} for _ in nodes]
    copies = [0] * (LAYERS * CHUNKS)
    for u, (x, z, q) in enumerate(nodes):
        layer = z // NK * NX + x
        for c in range(CHUNKS):
            held[u][layer * CHUNKS + c] = 0
            copies[layer * CHUNKS + c] += 1
    missing = count * LAYERS * CHUNKS - sum(len(h) for h in held)
    sends, ready = [], [0] * LAYERS
    while missing:
        r = len(sends)
        row = [[NONE] * LINKS for _ in nodes]
        turns = [(u, o) for u in range(count) for o in range(LINKS)]
        rnd.shuffle(turns)
        now = list(copies)
        for u, o in turns:
            there = held[goes[u][o]]
            best, best_key = None, None
            for c, when in held[u].items():
                if when <= r and c not in there:
                    key = c // CHUNKS * ORDER_WEIGHT + now[c] / count * RARE_WEIGHT + rnd.random() * NOISE
                    if best_key is None or key < best_key:
                        best, best_key = c, key
            if best is not None:
                there[best] = r + LAG
                copies[best] += 1
                missing -= 1
                ready[best // CHUNKS] = max(ready[best // CHUNKS], r + LAG)
                row[u][o] = best % CHUNKS * LAYERS + best // CHUNKS
        sends.append(row)
    return nodes, goes, sends, ready


def route_tables():
    nodes, goes, sends, ready = plan_routes()
    rounds = len(sends) + LAG
    back = [1, 0, 3, 2, 4]
    out_table = [[[NONE] * LINKS for _ in nodes] for _ in range(rounds)]
    in_table = [[[NONE] * LINKS for _ in nodes] for _ in range(rounds)]
    for r, row in enumerate(sends):
        for u in range(len(nodes)):
            for o in range(LINKS):
                out_table[r][u][o] = row[u][o]
                in_table[r + LAG][goes[u][o]][back[o]] = row[u][o]
    return nodes, out_table, in_table, ready


def step_rounds(ready):
    starts, last = [], -1
    for layer in range(LAYERS):
        for half in range(2):
            last = max(last + 1, ready[layer] + (1 if half == 0 else 0))
            starts.append(last)
    starts += [last + 1, last + 2]
    return starts


def kernel(
    tables, v_hbm, u_hbm, c_hbm, e_hbm, feat_hbm, out_hbm,
    W, E, X0, XC, ACC, DACC, PS, PR, DS, DR, T_OUT, T_IN,
    local_sem, w_recv, e_recv, wd_recv, ed_recv, w_send, e_send, wd_send, ed_send,
    x_sem, p_send, p_recv, d_send, d_recv, o_local, o_send, o_recv,
):
    nodes, out_table, in_table, ready = tables
    rounds = len(out_table)
    starts = step_rounds(ready)
    total = max(rounds, starts[-1] + 1)
    rows, half = X0.shape[1], X0.shape[2]
    sub_cols, piece = half // 2, half // 4
    rank = piece // 2

    sec = lax.axis_index("section")
    dp = lax.axis_index("dp")
    x, h = sec % NX, sec // NX
    core, y, k = dp % 2, dp // 2 % NY, dp // (2 * NY)
    z = h * NK + k
    q = 1 - y % 2
    p = (y + 1) // 2 % 2
    mine = y % 2
    pair_y = y + 1 - 2 * mine
    share_y = (y + 1 - 2 * q + NY) % NY

    def device(x_, z_, y_, core_):
        return (z_ // NK * NX + x_, (z_ % NK * NY + y_) * 2 + core_)

    targets = [
        device((x + 1) % NX, z, y, core), device((x + NX - 1) % NX, z, y, core),
        device(x, (z + 1) % NZ, y, core), device(x, (z + NZ - 1) % NZ, y, core),
        device(x, z, share_y, core),
    ]
    pair = device(x, z, pair_y, core)
    sibling = device(x, z, y, 1 - core)

    def local(src, dst, sem):
        return pltpu.make_async_copy(src, dst, sem)

    def remote(src, dst, send, recv, to):
        return pltpu.make_async_remote_copy(
            src_ref=src, dst_ref=dst, send_sem=send, recv_sem=recv, device_id=to, device_id_type=MESH
        )

    def arrived(ref, sem):
        pltpu.make_async_copy(ref, ref, sem).wait()

    barrier = pltpu.get_barrier_semaphore()
    for to in targets + [pair, sibling]:
        pl.semaphore_signal(barrier, inc=1, device_id=to, device_id_type=MESH)

    base = pl.multiple_of(p * half, half)
    other = pl.multiple_of((1 - p) * half, half)
    own = []
    for s in range(2):
        for j in range(8):
            own.append(local(
                v_hbm.at[0, pl.ds(pl.multiple_of(base + s * sub_cols + j * 128, 128), 128), :],
                W.at[s, j, sec], local_sem.at[s, j]))
            b, a = j // 4, j % 4
            own.append(local(
                u_hbm.at[0, a * 128:(a + 1) * 128, pl.ds(pl.multiple_of(base + s * sub_cols + b * piece, piece), piece)],
                W.at[s, 8 + j, sec], local_sem.at[s, 8 + j]))
        own.append(local(c_hbm.at[s], W.at[s, 16, sec], local_sem.at[s, 16]))
        own.append(local(e_hbm.at[s], E.at[s, sec], local_sem.at[s, 17]))
    for copy in own:
        copy.start()
    x_local = local(feat_hbm.at[0, 0, :, pl.ds(base, half)], X0.at[mine], x_sem.at[0])
    x_local.start()

    bits = [x % 2 == 1, x // 2 == 1, h == 1, q == 1]
    shift = k * 8

    def lookup(table, r, o):
        values = {n: table[r][i][o] for i, n in enumerate(nodes)}
        words = []
        for cls in range(16):
            x_, h_, q_ = cls % 4, cls // 4 % 2, cls // 8
            word = 0
            for k_ in range(NK):
                word |= values[(x_, h_ * NK + k_, q_)] << (8 * k_)
            words.append(word - (1 << 32) if word >= 1 << 31 else word)
        level = words
        for bit in bits:
            level = [
                level[i] if isinstance(level[i], int) and isinstance(level[i + 1], int) and level[i] == level[i + 1]
                else jnp.where(bit, jnp.int32(level[i + 1]), jnp.int32(level[i]))
                for i in range(0, len(level), 2)
            ]
        word = level[0]
        if isinstance(word, int):
            word = jnp.int32(word)
        return lax.shift_right_logical(word, shift) & 255

    for r in range(rounds):
        for o in range(LINKS):
            T_OUT[r * LINKS + o] = lookup(out_table, r, o)
            T_IN[r * LINKS + o] = lookup(in_table, r, o)

    pl.semaphore_wait(barrier, LINKS + 2)
    x_remote = remote(feat_hbm.at[0, 0, :, pl.ds(other, half)], X0.at[mine], x_sem.at[1], x_sem.at[2], pair)
    x_remote.start()
    for copy in own:
        copy.wait()

    def settle(send_w, send_e, slot, ident):
        @pl.when(ident != NONE)
        def _():
            j, l = ident // LAYERS, ident % LAYERS
            arrived(W.at[core, j, l], send_w.at[slot])

            @pl.when(j == 16)
            def _():
                arrived(E.at[core, l], send_e.at[slot])

    def push(ident, slot, send_w, send_e, recv_w, recv_e, to):
        j, l = ident // LAYERS, ident % LAYERS
        remote(W.at[core, j, l], W.at[core, j, l], send_w.at[slot], recv_w.at[j, l], to).start()

        @pl.when(j == 16)
        def _():
            remote(E.at[core, l], E.at[core, l], send_e.at[slot], recv_e.at[l], to).start()

    def traffic(r):
        slot0 = r % SLOTS * LINKS

        @pl.when(r >= SLOTS)
        def _():
            for o in range(LINKS):
                settle(w_send, e_send, slot0 + o, T_OUT[(r - SLOTS) * LINKS + o])
                settle(wd_send, ed_send, slot0 + o, T_IN[(r - SLOTS) * LINKS + o])

        for o in range(LINKS):
            ident = T_IN[r * LINKS + o]

            @pl.when(ident != NONE)
            def _():
                j, l = ident // LAYERS, ident % LAYERS
                arrived(W.at[core, j, l], w_recv.at[j, l])

                @pl.when(j == 16)
                def _():
                    arrived(E.at[core, l], e_recv.at[l])

                push(ident, slot0 + o, wd_send, ed_send, wd_recv, ed_recv, sibling)

        for o in range(LINKS):
            ident_out = T_OUT[r * LINKS + o]

            @pl.when(ident_out != NONE)
            def _():
                push(ident_out, slot0 + o, w_send, e_send, w_recv, e_recv, targets[o])

    def weights_here(l):
        @pl.when(l != sec)
        def _():
            def one(j, carry):
                arrived(W.at[1 - core, j, l], wd_recv.at[j, l])
                return carry
            lax.fori_loop(0, CHUNKS, one, 0)
            arrived(E.at[1 - core, l], ed_recv.at[l])

    def project(l, s):
        acc = jnp.zeros((rows, piece), jnp.float32)
        mixed = jnp.zeros((rows, piece), jnp.float32)
        for sub in range(2):
            part = XC[s, :, sub * sub_cols:(sub + 1) * sub_cols]
            v_mat = W[sub, 0:8, l].reshape(sub_cols, piece)
            acc = acc + jnp.dot(part, v_mat, preferred_element_type=jnp.float32)
            for b in range(2):
                block = part[:, b * piece:(b + 1) * piece].astype(jnp.float32)
                mixed = mixed + block * E[sub, l, 2 + b:3 + b, :]
        ACC[s] = acc
        PS[l, s] = acc.astype(jnp.bfloat16)
        lanes = mixed[:, 0:128] + mixed[:, 128:256] + mixed[:, 256:384] + mixed[:, 384:512]
        logit = jnp.broadcast_to(jnp.sum(lanes, axis=1, keepdims=True), (rows, 128))
        DACC[s] = logit
        DS[l, s] = logit.T[0:8, :]
        remote(PS.at[l, s], PR.at[l, s], p_send.at[l, s], p_recv.at[l, s], pair).start()
        remote(DS.at[l, s], DR.at[l, s], d_send.at[l, s], d_recv.at[l, s], pair).start()

    def finish(l, s):
        arrived(PR.at[l, s], p_recv.at[l, s])
        arrived(DR.at[l, s], d_recv.at[l, s])
        first = jnp.tanh(ACC[s] + PR[l, s].astype(jnp.float32)).astype(jnp.bfloat16)
        logit = DACC[s] + jnp.broadcast_to(DR[l, s][0:1, :], (128, rows)).T
        gates = (1.0 / (1.0 + jnp.exp(-logit)), 1.0 / (1.0 + jnp.exp(logit)))
        c_mat = W[:, 16, l].reshape(rank, piece)
        parts = []
        for i in range(2):
            cols = slice(i * rank, (i + 1) * rank)
            second = jnp.dot(first[:, cols], c_mat[:, cols], preferred_element_type=jnp.float32)
            gate = jnp.concatenate([gates[i], gates[i]], axis=1)
            parts.append((gate * jnp.tanh(second)).astype(jnp.bfloat16))
        blended = jnp.concatenate(parts, axis=1)
        for sub in range(2):
            for b in range(2):
                u_mat = W[sub, 8 + 4 * b:12 + 4 * b, l].reshape(piece, piece)
                cross = jnp.dot(blended, u_mat, preferred_element_type=jnp.float32)
                at = sub * sub_cols + b * piece
                cols = slice(at, at + piece)
                new = XC[s, :, cols].astype(jnp.float32) + X0[s, :, cols].astype(jnp.float32) * (
                    cross + E[sub, l, b:b + 1, :])
                XC[s, :, cols] = new.astype(jnp.bfloat16)

                @pl.when(l == LAYERS - 1)
                def _():
                    j = sub * 2 + b
                    dst = out_hbm.at[0, 0, :, pl.ds(pl.multiple_of(base + at, piece), piece)]

                    @pl.when(s == mine)
                    def _():
                        local(XC.at[s, :, cols], dst, o_local.at[j]).start()

                    @pl.when(s != mine)
                    def _():
                        remote(XC.at[s, :, cols], dst, o_send.at[j], o_recv.at[j], pair).start()

    def one_round(r, carry):
        @pl.when(r < rounds)
        def _():
            traffic(r)

        step = jnp.int32(-1)
        fires = jnp.int32(0)
        for start in starts:
            step = step + jnp.where(r >= start, 1, 0)
            fires = fires + jnp.where(r == start, 1, 0)

        @pl.when(fires > 0)
        def _():
            l, s = step // 2, step % 2

            @pl.when(step == 0)
            def _():
                x_local.wait()
                x_remote.wait_send()
                arrived(X0.at[1 - mine], x_sem.at[2])
                XC[...] = X0[...]

            @pl.when(step >= 2)
            def _():
                finish(l - 1, s)

            @pl.when(l < LAYERS)
            def _():
                @pl.when(s == 0)
                def _():
                    weights_here(l)
                project(l, s)

        return carry

    lax.fori_loop(0, total, one_round, 0)

    for r in range(max(rounds - SLOTS, 0), rounds):
        for o in range(LINKS):
            slot = r % SLOTS * LINKS + o
            settle(w_send, e_send, slot, T_OUT[r * LINKS + o])
            settle(wd_send, ed_send, slot, T_IN[r * LINKS + o])

    def sent(i, carry):
        l, s = i // 2, i % 2
        arrived(PS.at[l, s], p_send.at[l, s])
        arrived(DS.at[l, s], d_send.at[l, s])
        return carry

    lax.fori_loop(0, LAYERS * 2, sent, 0)
    for j in range(4):
        at = j * piece
        cols = slice(at, at + piece)
        mine_dst = out_hbm.at[0, 0, :, pl.ds(pl.multiple_of(base + at, piece), piece)]
        pair_dst = out_hbm.at[0, 0, :, pl.ds(pl.multiple_of(other + at, piece), piece)]
        local(XC.at[mine, :, cols], mine_dst, o_local.at[j]).wait()
        arrived(XC.at[1 - mine, :, cols], o_send.at[j])
        arrived(pair_dst, o_recv.at[j])


def per_device(features, in_proj, mix_proj, out_proj, gate_proj, cross_bias):
    rows, width = features.shape[2], features.shape[3]
    experts, rank = mix_proj.shape[1], mix_proj.shape[2]
    half, piece = width // 2, experts * rank
    y = lax.axis_index("dp") // 2 % NY
    p = (y + 1) // 2 % 2

    def own_half(vector):
        return lax.dynamic_slice_in_dim(vector.reshape(2, 2, 2, piece), p, 1, axis=0)[0]

    gate = gate_proj[0].astype(jnp.float32)
    extra = jnp.concatenate(
        [own_half(cross_bias[0]), own_half(gate[0] - gate[1]), jnp.zeros((2, 4, piece), jnp.float32)], axis=1
    )
    mix = mix_proj[0].transpose(1, 0, 2).reshape(2, rank // 2, piece)
    tables = route_tables()
    rounds = len(tables[1])
    any_space = pl.BlockSpec(memory_space=pl.ANY)
    dma = pltpu.SemaphoreType.DMA
    return pl.pallas_call(
        functools.partial(kernel, tables),
        out_shape=jax.ShapeDtypeStruct(features.shape, features.dtype),
        in_specs=[any_space] * 5,
        out_specs=any_space,
        scratch_shapes=[
            pltpu.VMEM((2, CHUNKS, LAYERS, 128, piece), jnp.bfloat16),
            pltpu.VMEM((2, LAYERS, 8, piece), jnp.float32),
            pltpu.VMEM((2, rows, half), jnp.bfloat16),
            pltpu.VMEM((2, rows, half), jnp.bfloat16),
            pltpu.VMEM((2, rows, piece), jnp.float32),
            pltpu.VMEM((2, rows, 128), jnp.float32),
            pltpu.VMEM((LAYERS, 2, rows, piece), jnp.bfloat16),
            pltpu.VMEM((LAYERS, 2, rows, piece), jnp.bfloat16),
            pltpu.VMEM((LAYERS, 2, 8, rows), jnp.float32),
            pltpu.VMEM((LAYERS, 2, 8, rows), jnp.float32),
            pltpu.SMEM((rounds * LINKS,), jnp.int32),
            pltpu.SMEM((rounds * LINKS,), jnp.int32),
            dma((2, 18)),
            dma((CHUNKS, LAYERS)), dma((LAYERS,)),
            dma((CHUNKS, LAYERS)), dma((LAYERS,)),
            dma((SLOTS * LINKS,)), dma((SLOTS * LINKS,)),
            dma((SLOTS * LINKS,)), dma((SLOTS * LINKS,)),
            dma((3,)),
            dma((LAYERS, 2)), dma((LAYERS, 2)), dma((LAYERS, 2)), dma((LAYERS, 2)),
            dma((4,)), dma((4,)), dma((4,)),
        ],
        compiler_params=pltpu.CompilerParams(
            collective_id=0, has_side_effects=True, vmem_limit_bytes=60 * 1024 * 1024
        ),
    )(in_proj, out_proj, mix, extra, features)


def solution(mesh):
    placed = (
        P(None, "section", "dp", None),
        P("section", None, None),
        P("section", None, None, None),
        P("section", None, None),
        P("section", None, None),
        P("section", None),
    )
    return jax.shard_map(
        per_device,
        mesh=mesh,
        in_specs=placed,
        out_specs=P(None, "section", "dp", None),
        check_vma=False,
    )
```

time: 970 us -> 136 us (0.14)
  the two profiles are of different devices: /device:TPU:160 before, /device:TPU:8 now
where the time goes in v1:
time: 136 us
  Pallas kernels  128 us (94%)
  local copies, waits for them, and re-layouts  5.01 us (4%)
  other arithmetic  2.86 us (2%)
    pallas_call x1, Pallas kernels, per_device(): pl.pallas_call(functools.partial(kernel, tables), out_shape=jax.ShapeDtyp...  128 us
    unnamed x2, local copies, waits for them, and re-layouts  2.8 us

profile of v1, /device:TPU:8, one launch (start us, length us, event | category | flops | bytes accessed | tf_op | source)
XLA Modules:
  0.0 135.8 jit_solution(18289514692966382739)
XLA Ops:
  0.0 0.1 pad.2.clone
  0.1 0.5 broadcast.12
  0.6 1.4 %reduce.7 = f32[4096]{0:T(1024)S(1)} reduce(f32[1,4096]{1,0:T(1,128)} %param.11, f32[]{:T(128)} %broadcast.12), dimensions={0}, to_apply=%param.11.reduce_sub_computation.3 | reduce | bytes 32772 | tf_op args[5]
  2.0 0.7 convert_element_type.4
  2.8 0.1 fusion
  2.8 0.7 maximum_maximum_fusion.e_hbm
  3.5 1.2 copy.7
  4.7 0.9 reshape.12.c_hbm
  5.6 127.8 %shard_map.64 = bf16[1,1,128,4096]{3,2,1,0:T(8,128)(2,1)} custom-call(bf16[1,4096,512]{2,1,0:T(8,128)(2,1)} %v_hbm.1, bf16[1,512,4096]{2,1,0:T(8,128)(2,1)} %u_hbm.1, bf16[2,128,512]{2,1,0:T(8,128)(2,1)} %reshape.12.c_hbm, f32[2,8,512]{2,1,0:T(8,128)} %maximum_maximum_fusion.e_hbm, bf16[1,1,128,4096]{3,2,1,0:T(8,128)(2,1)} %feat_hbm.1), custom_call_target="tpu_custom_call" | custom-call | tf_op jit(solution)/shard_map/pallas_call | solution.py:388
  133.5 2.3 %copy.9 = bf16[1,1,128,4096]{3,2,1,0:T(8,128)(2,1)} copy(bf16[1,1,128,4096]{3,2,1,0:T(8,128)(2,1)} %shard_map.64) | data formatting | bytes 2097152
  (4 shorter events, 0.0 us)

commit v2 on v1

v2 whole, which is shorter than its diff:
```python
import functools
import random

import jax
import jax.numpy as jnp
from jax import lax
from jax.experimental import pallas as pl
from jax.experimental.pallas import tpu as pltpu
from jax.sharding import PartitionSpec as P

MESH = pl.DeviceIdType.MESH
NX, NH, NK, NY, NQ = 4, 2, 4, 4, 2
NZ = NH * NK
LAYERS = NX * NH
PART = 128
NV = 1024 // PART
NC = 128 // PART
CHUNKS = 2 * NV + NC
LINKS = 5
LAG = 2
PACE, GAP = 1, 1
SLOTS = 4
NONE = 4095
ROUTE = (0.8, 4, 0.3, 3600, 2, 2)


def chunk_groups():
    first = list(range(NV)) + list(range(2 * NV, CHUNKS))
    return first, list(range(NV, NV + NV // 2)), list(range(NV + NV // 2, 2 * NV))


def plan_routes(order_weight, rare_weight, noise, seed, late, last):
    rnd = random.Random(seed)
    nodes = [(x, z, q) for x in range(NX) for z in range(NZ) for q in range(NQ)]
    index = {n: i for i, n in enumerate(nodes)}
    count = len(nodes)
    goes = []
    for x, z, q in nodes:
        goes.append([
            index[((x + 1) % NX, z, q)], index[((x - 1) % NX, z, q)],
            index[(x, (z + 1) % NZ, q)], index[(x, (z - 1) % NZ, q)], index[(x, z, 1 - q)],
        ])
    _, second, third = chunk_groups()
    due = []
    for c in range(LAYERS * CHUNKS):
        layer, part = divmod(c, CHUNKS)
        steps = 2 * layer + (late if part in second + third else 0)
        if layer == LAYERS - 1 and part in third:
            steps += last
        due.append(steps * order_weight / 2)
    held = [{} for _ in nodes]
    copies = [0] * (LAYERS * CHUNKS)
    for u, (x, z, q) in enumerate(nodes):
        layer = z // NK * NX + x
        for c in range(CHUNKS):
            held[u][layer * CHUNKS + c] = 0
            copies[layer * CHUNKS + c] += 1
    missing = count * LAYERS * CHUNKS - sum(len(h) for h in held)
    sends, ready = [], [0] * (LAYERS * CHUNKS)
    while missing:
        r = len(sends)
        row = [[NONE] * LINKS for _ in nodes]
        turns = [(u, o) for u in range(count) for o in range(LINKS)]
        rnd.shuffle(turns)
        base = [due[c] + copies[c] / count * rare_weight for c in range(LAYERS * CHUNKS)]
        for u, o in turns:
            there = held[goes[u][o]]
            best, best_key = None, None
            for c, when in held[u].items():
                if when <= r and c not in there:
                    key = base[c] + rnd.random() * noise
                    if best_key is None or key < best_key:
                        best, best_key = c, key
            if best is not None:
                there[best] = r + LAG
                copies[best] += 1
                missing -= 1
                ready[best] = max(ready[best], r + LAG)
                row[u][o] = best % CHUNKS * LAYERS + best // CHUNKS
        sends.append(row)
    return nodes, goes, sends, ready


def route_tables():
    nodes, goes, sends, ready = plan_routes(*ROUTE)
    rounds = len(sends) + LAG
    back = [1, 0, 3, 2, 4]
    out_table = [[[NONE] * LINKS for _ in nodes] for _ in range(rounds)]
    in_table = [[[NONE] * LINKS for _ in nodes] for _ in range(rounds)]
    for r, row in enumerate(sends):
        for u in range(len(nodes)):
            for o in range(LINKS):
                out_table[r][u][o] = row[u][o]
                in_table[r + LAG][goes[u][o]][back[o]] = row[u][o]
    return nodes, out_table, in_table, step_rounds(ready)


def step_rounds(ready):
    def last_of(layer, group):
        return max(ready[layer * CHUNKS + c] for c in group)

    first, second, third = chunk_groups()
    pace, gap = PACE, GAP
    starts, at = [], -pace
    for layer in range(LAYERS):
        need = last_of(layer, first) + gap
        if layer:
            need = max(need, last_of(layer - 1, second + third) + gap)
        at = max(at + pace, need)
        starts.append(at)
        at += pace
        starts.append(at)
    starts += [at + pace, at + 2 * pace]
    at = max(at + 2 * pace + 1, last_of(LAYERS - 1, second) + gap)
    starts.append(at)
    starts.append(max(at + 1, last_of(LAYERS - 1, third) + gap))
    return starts


def kernel(
    tables, v_hbm, u_hbm, c_hbm, gate_ref, bias_ref, feat_hbm, out_hbm,
    W, E, X0, XC, ACC, DACC, BL, PS, PR, DS, DR, T_OUT, T_IN,
    local_sem, w_recv, e_recv, wd_recv, ed_recv, w_send, e_send, wd_send, ed_send,
    x_sem, p_send, p_recv, d_send, d_recv, o_local, o_send, o_recv,
):
    nodes, out_table, in_table, starts = tables
    rounds = len(out_table)
    total = max(rounds, starts[-1] + 1)
    rows, half = X0.shape[1], X0.shape[2]
    sub_cols, piece = half // 2, half // 4
    rank = piece // 2
    block = rows // 2
    deep = piece // PART

    sec = lax.axis_index("section")
    dp = lax.axis_index("dp")
    x, h = sec % NX, sec // NX
    core, y, k = dp % 2, dp // 2 % NY, dp // (2 * NY)
    z = h * NK + k
    q = 1 - y % 2
    p = (y + 1) // 2 % 2
    mine = y % 2
    pair_y = y + 1 - 2 * mine
    share_y = (y + 1 - 2 * q + NY) % NY

    def device(x_, z_, y_, core_):
        return (z_ // NK * NX + x_, (z_ % NK * NY + y_) * 2 + core_)

    targets = [
        device((x + 1) % NX, z, y, core), device((x + NX - 1) % NX, z, y, core),
        device(x, (z + 1) % NZ, y, core), device(x, (z + NZ - 1) % NZ, y, core),
        device(x, z, share_y, core),
    ]
    pair = device(x, z, pair_y, core)
    sibling = device(x, z, y, 1 - core)

    def local(src, dst, sem):
        return pltpu.make_async_copy(src, dst, sem)

    def remote(src, dst, send, recv, to):
        return pltpu.make_async_remote_copy(
            src_ref=src, dst_ref=dst, send_sem=send, recv_sem=recv, device_id=to, device_id_type=MESH
        )

    def arrived(ref, sem):
        pltpu.make_async_copy(ref, ref, sem).wait()

    barrier = pltpu.get_barrier_semaphore()
    for to in targets + [pair, sibling]:
        pl.semaphore_signal(barrier, inc=1, device_id=to, device_id_type=MESH)

    base = pl.multiple_of(p * half, half)
    other = pl.multiple_of((1 - p) * half, half)
    own = []
    for s in range(2):
        for j in range(NV):
            own.append(local(
                v_hbm.at[0, pl.ds(pl.multiple_of(base + s * sub_cols + j * PART, PART), PART), :],
                W.at[s, j, sec], local_sem.at[s, j]))
            b, a = j // deep, j % deep
            own.append(local(
                u_hbm.at[0, a * PART:(a + 1) * PART, pl.ds(pl.multiple_of(base + s * sub_cols + b * piece, piece), piece)],
                W.at[s, NV + j, sec], local_sem.at[s, NV + j]))
        for j in range(NC):
            for e in range(2):
                own.append(local(
                    c_hbm.at[0, e, s * 128 + j * PART:s * 128 + (j + 1) * PART, :],
                    W.at[s, 2 * NV + j, sec, :, e * rank:(e + 1) * rank], local_sem.at[s, 2 * NV + 2 * j + e]))
    for copy in own:
        copy.start()
    x_local = [
        local(feat_hbm.at[0, 0, s * block:(s + 1) * block, pl.ds(base, half)],
              X0.at[s, pl.ds(pl.multiple_of(mine * block, block), block), :], x_sem.at[s])
        for s in range(2)
    ]
    for copy in x_local:
        copy.start()
    for s in range(2):
        extra = []
        for ref in (bias_ref, gate_ref):
            for b in range(2):
                cols = pl.ds(pl.multiple_of(base + s * sub_cols + b * piece, piece), piece)
                if ref is bias_ref:
                    extra.append(ref[0:1, cols])
                else:
                    both = ref[0, :, cols].astype(jnp.float32)
                    extra.append(both[0:1, :] - both[1:2, :])
        extra.append(jnp.zeros((4, piece), jnp.float32))
        E[s, sec] = jnp.concatenate(extra, axis=0)

    bits = [x % 2 == 1, x // 2 == 1, h == 1, q == 1, k // 2 == 1]
    shift = k % 2 * 16

    def lookup(table, r, o):
        values = {n: table[r][i][o] for i, n in enumerate(nodes)}
        level = []
        for cls in range(32):
            x_, h_, q_, k_ = cls % 4, cls // 4 % 2, cls // 8 % 2, cls // 16 * 2
            level.append(values[(x_, h_ * NK + k_, q_)] + (values[(x_, h_ * NK + k_ + 1, q_)] << 16))
        for bit in bits:
            level = [
                level[i] if isinstance(level[i], int) and isinstance(level[i + 1], int) and level[i] == level[i + 1]
                else jnp.where(bit, jnp.int32(level[i + 1]), jnp.int32(level[i]))
                for i in range(0, len(level), 2)
            ]
        word = level[0]
        if isinstance(word, int):
            word = jnp.int32(word)
        return lax.shift_right_logical(word, shift) & 4095

    for r in range(rounds):
        for o in range(LINKS):
            T_OUT[r * LINKS + o] = lookup(out_table, r, o)
            T_IN[r * LINKS + o] = lookup(in_table, r, o)

    pl.semaphore_wait(barrier, LINKS + 2)
    x_remote = [
        remote(feat_hbm.at[0, 0, s * block:(s + 1) * block, pl.ds(other, half)],
               X0.at[s, pl.ds(pl.multiple_of(mine * block, block), block), :], x_sem.at[2 + s], x_sem.at[4 + s], pair)
        for s in range(2)
    ]
    for copy in x_remote:
        copy.start()
    for copy in own:
        copy.wait()

    def settle(send_w, send_e, slot, ident):
        @pl.when(ident != NONE)
        def _():
            j, l = ident // LAYERS, ident % LAYERS
            arrived(W.at[core, j, l], send_w.at[slot])

            @pl.when(j == 2 * NV)
            def _():
                arrived(E.at[core, l], send_e.at[slot])

    def push(ident, slot, send_w, send_e, recv_w, recv_e, to):
        j, l = ident // LAYERS, ident % LAYERS
        remote(W.at[core, j, l], W.at[core, j, l], send_w.at[slot], recv_w.at[j, l], to).start()

        @pl.when(j == 2 * NV)
        def _():
            remote(E.at[core, l], E.at[core, l], send_e.at[slot], recv_e.at[l], to).start()

    def traffic(r):
        slot0 = r % SLOTS * LINKS

        @pl.when(r >= SLOTS)
        def _():
            for o in range(LINKS):
                settle(w_send, e_send, slot0 + o, T_OUT[(r - SLOTS) * LINKS + o])
                settle(wd_send, ed_send, slot0 + o, T_IN[(r - SLOTS) * LINKS + o])

        for o in range(LINKS):
            ident = T_IN[r * LINKS + o]

            @pl.when(ident != NONE)
            def _():
                j, l = ident // LAYERS, ident % LAYERS
                arrived(W.at[core, j, l], w_recv.at[j, l])

                @pl.when(j == 2 * NV)
                def _():
                    arrived(E.at[core, l], e_recv.at[l])

                push(ident, slot0 + o, wd_send, ed_send, wd_recv, ed_recv, sibling)

        for o in range(LINKS):
            ident_out = T_OUT[r * LINKS + o]

            @pl.when(ident_out != NONE)
            def _():
                push(ident_out, slot0 + o, w_send, e_send, w_recv, e_recv, targets[o])

    def weights_here(l, low, high, extra=False):
        @pl.when(l != sec)
        def _():
            def one(j, carry):
                arrived(W.at[1 - core, j, l], wd_recv.at[j, l])
                return carry
            lax.fori_loop(low, high, one, 0)
            if extra:
                arrived(E.at[1 - core, l], ed_recv.at[l])

    def project(l, s):
        acc = jnp.zeros((rows, piece), jnp.float32)
        mixed = jnp.zeros((rows, piece), jnp.float32)
        for sub in range(2):
            part = XC[s, :, sub * sub_cols:(sub + 1) * sub_cols]
            v_mat = W[sub, 0:NV, l].reshape(sub_cols, piece)
            acc = acc + jnp.dot(part, v_mat, preferred_element_type=jnp.float32)
            for b in range(2):
                cut = part[:, b * piece:(b + 1) * piece].astype(jnp.float32)
                mixed = mixed + cut * E[sub, l, 2 + b:3 + b, :]
        ACC[s] = acc
        PS[l, s] = acc.astype(jnp.bfloat16)
        lanes = mixed[:, 0:128] + mixed[:, 128:256] + mixed[:, 256:384] + mixed[:, 384:512]
        logit = jnp.broadcast_to(jnp.sum(lanes, axis=1, keepdims=True), (rows, 128))
        DACC[s] = logit
        DS[l, s] = logit.T[0:8, :]
        remote(PS.at[l, s], PR.at[l, s], p_send.at[l, s], p_recv.at[l, s], pair).start()
        remote(DS.at[l, s], DR.at[l, s], d_send.at[l, s], d_recv.at[l, s], pair).start()

    def blend(l, s):
        arrived(PR.at[l, s], p_recv.at[l, s])
        arrived(DR.at[l, s], d_recv.at[l, s])
        first = jnp.tanh(ACC[s] + PR[l, s].astype(jnp.float32)).astype(jnp.bfloat16)
        logit = DACC[s] + jnp.broadcast_to(DR[l, s][0:1, :], (128, rows)).T
        gates = (1.0 / (1.0 + jnp.exp(-logit)), 1.0 / (1.0 + jnp.exp(logit)))
        c_mat = W[:, 2 * NV:CHUNKS, l].reshape(rank, piece)
        parts = []
        for i in range(2):
            cols = slice(i * rank, (i + 1) * rank)
            second = jnp.dot(first[:, cols], c_mat[:, cols], preferred_element_type=jnp.float32)
            gate = jnp.concatenate([gates[i], gates[i]], axis=1)
            parts.append((gate * jnp.tanh(second)).astype(jnp.bfloat16))
        return jnp.concatenate(parts, axis=1)

    def expand(blended, l, s, sub, b):
        u_mat = W[sub, pl.ds(NV + deep * b, deep), l].reshape(piece, piece)
        cross = jnp.dot(blended, u_mat, preferred_element_type=jnp.float32)
        cols = pl.ds(pl.multiple_of(sub * sub_cols + b * piece, piece), piece)
        new = XC[s, :, cols].astype(jnp.float32) + X0[s, :, cols].astype(jnp.float32) * (
            cross + E[sub, l, pl.ds(b, 1), :])
        XC[s, :, cols] = new.astype(jnp.bfloat16)

    def finish(l, s):
        blended = blend(l, s)
        for sub in range(2):
            for b in range(2):
                expand(blended, l, s, sub, b)

    def results(b, s, sub):
        at = sub * sub_cols + b * piece
        src = pl.ds(pl.multiple_of(at, piece), piece)
        dst = out_hbm.at[0, 0, s * block:(s + 1) * block, pl.ds(pl.multiple_of(base + at, piece), piece)]
        slot = b * 4 + s * 2 + sub
        return (
            local(XC.at[s, pl.ds(pl.multiple_of(mine * block, block), block), src], dst, o_local.at[slot]),
            remote(XC.at[s, pl.ds(pl.multiple_of((1 - mine) * block, block), block), src], dst,
                   o_send.at[slot], o_recv.at[slot], pair),
        )

    def one_round(r, carry):
        @pl.when(r < rounds)
        def _():
            traffic(r)

        step = jnp.int32(-1)
        fires = jnp.int32(0)
        for start in starts:
            step = step + jnp.where(r >= start, 1, 0)
            fires = fires + jnp.where(r == start, 1, 0)

        @pl.when((fires > 0) & (step < 2 * LAYERS))
        def _():
            l, s = step // 2, step % 2

            @pl.when(step == 0)
            def _():
                for copy in x_local:
                    copy.wait()
                for s_ in range(2):
                    x_remote[s_].wait_send()
                    arrived(X0.at[s_, pl.ds(pl.multiple_of((1 - mine) * block, block), block), :], x_sem.at[4 + s_])
                XC[...] = X0[...]

            @pl.when(step >= 2)
            def _():
                @pl.when(s == 0)
                def _():
                    weights_here(l - 1, NV, 2 * NV)
                finish(l - 1, s)

            @pl.when(s == 0)
            def _():
                weights_here(l, 0, NV)
                weights_here(l, 2 * NV, CHUNKS, True)
            project(l, s)

        @pl.when((fires > 0) & (step >= 2 * LAYERS) & (step < 2 * LAYERS + 2))
        def _():
            BL[step % 2] = blend(LAYERS - 1, step % 2)

        @pl.when((fires > 0) & (step >= 2 * LAYERS + 2))
        def _():
            b = step % 2
            low = NV + b * (NV // 2)
            weights_here(LAYERS - 1, low, low + NV // 2)
            for s in range(2):
                for sub in range(2):
                    expand(BL[s], LAYERS - 1, s, sub, b)
                    for copy in results(b, s, sub):
                        copy.start()

        return carry

    lax.fori_loop(0, total, one_round, 0)

    for r in range(max(rounds - SLOTS, 0), rounds):
        for o in range(LINKS):
            slot = r % SLOTS * LINKS + o
            settle(w_send, e_send, slot, T_OUT[r * LINKS + o])
            settle(wd_send, ed_send, slot, T_IN[r * LINKS + o])

    def sent(i, carry):
        l, s = i // 2, i % 2
        arrived(PS.at[l, s], p_send.at[l, s])
        arrived(DS.at[l, s], d_send.at[l, s])
        return carry

    lax.fori_loop(0, LAYERS * 2, sent, 0)
    for b in range(2):
        for s in range(2):
            for sub in range(2):
                here, there = results(b, s, sub)
                here.wait()
                there.wait_send()
                at = sub * sub_cols + b * piece
                arrived(out_hbm.at[0, 0, s * block:(s + 1) * block, pl.ds(pl.multiple_of(other + at, piece), piece)],
                        o_recv.at[b * 4 + s * 2 + sub])


def per_device(features, in_proj, mix_proj, out_proj, gate_proj, cross_bias):
    rows, width = features.shape[2], features.shape[3]
    experts, rank = mix_proj.shape[1], mix_proj.shape[2]
    half, piece = width // 2, experts * rank
    tables = route_tables()
    rounds = len(tables[1])
    any_space = pl.BlockSpec(memory_space=pl.ANY)
    dma = pltpu.SemaphoreType.DMA
    return pl.pallas_call(
        functools.partial(kernel, tables),
        out_shape=jax.ShapeDtypeStruct(features.shape, features.dtype),
        in_specs=[any_space] * 3 + [pl.BlockSpec(memory_space=pltpu.VMEM)] * 2 + [any_space],
        out_specs=any_space,
        scratch_shapes=[
            pltpu.VMEM((2, CHUNKS, LAYERS, PART, piece), jnp.bfloat16),
            pltpu.VMEM((2, LAYERS, 8, piece), jnp.float32),
            pltpu.VMEM((2, rows, half), jnp.bfloat16),
            pltpu.VMEM((2, rows, half), jnp.bfloat16),
            pltpu.VMEM((2, rows, piece), jnp.float32),
            pltpu.VMEM((2, rows, 128), jnp.float32),
            pltpu.VMEM((2, rows, piece), jnp.bfloat16),
            pltpu.VMEM((LAYERS, 2, rows, piece), jnp.bfloat16),
            pltpu.VMEM((LAYERS, 2, rows, piece), jnp.bfloat16),
            pltpu.VMEM((LAYERS, 2, 8, rows), jnp.float32),
            pltpu.VMEM((LAYERS, 2, 8, rows), jnp.float32),
            pltpu.SMEM((rounds * LINKS,), jnp.int32),
            pltpu.SMEM((rounds * LINKS,), jnp.int32),
            dma((2, CHUNKS + NC)),
            dma((CHUNKS, LAYERS)), dma((LAYERS,)),
            dma((CHUNKS, LAYERS)), dma((LAYERS,)),
            dma((SLOTS * LINKS,)), dma((SLOTS * LINKS,)),
            dma((SLOTS * LINKS,)), dma((SLOTS * LINKS,)),
            dma((6,)),
            dma((LAYERS, 2)), dma((LAYERS, 2)), dma((LAYERS, 2)), dma((LAYERS, 2)),
            dma((8,)), dma((8,)), dma((8,)),
        ],
        compiler_params=pltpu.CompilerParams(
            collective_id=0, has_side_effects=True, vmem_limit_bytes=60 * 1024 * 1024
        ),
    )(in_proj, out_proj, mix_proj, gate_proj, cross_bias, features)


def solution(mesh):
    placed = (
        P(None, "section", "dp", None),
        P("section", None, None),
        P("section", None, None, None),
        P("section", None, None),
        P("section", None, None),
        P("section", None),
    )
    return jax.shard_map(
        per_device,
        mesh=mesh,
        in_specs=placed,
        out_specs=P(None, "section", "dp", None),
        check_vma=False,
    )
```

time: 136 us -> 126 us (0.926)
  Pallas kernels: 128 us -> 123 us
  other arithmetic: 2.86 us -> 0 us
  local copies, waits for them, and re-layouts: 5.01 us -> 2.29 us
    pallas_call x1, Pallas kernels: 128 us -> 123 us  [per_device(): pl.pallas_call(functools.partial(kernel, tables), out_shape=jax.ShapeDtyp...]
    unnamed x1 -> x0, other arithmetic: 1.4 us -> none
    unnamed x2 -> x1, local copies, waits for them, and re-layouts: 2.8 us -> 2.29 us
where the time goes in v2:
time: 126 us
  Pallas kernels  123 us (98%)
  local copies, waits for them, and re-layouts  2.29 us (2%)
    pallas_call x1, Pallas kernels, per_device(): pl.pallas_call(functools.partial(kernel, tables), out_shape=jax.ShapeDtyp...  123 us

profile of v2, /device:TPU:8, one launch (start us, length us, event | category | flops | bytes accessed | tf_op | source)
XLA Modules:
  0.0 125.7 jit_solution(5651217999291554490)
XLA Ops:
  0.0 123.4 %shard_map.64 = bf16[1,1,128,4096]{3,2,1,0:T(8,128)(2,1)} custom-call(bf16[1,4096,512]{2,1,0:T(8,128)(2,1)} %v_hbm.1, bf16[1,512,4096]{2,1,0:T(8,128)(2,1)} %u_hbm.1, bf16[1,2,256,256]{3,2,1,0:T(8,128)(2,1)} %c_hbm.1, bf16[1,2,4096]{2,1,0:T(2,128)(2,1)} %gate_ref.1, f32[1,4096]{1,0:T(1,128)} %bias_ref.1, bf16[1,1,128,4096]{3,2,1,0:T(8,128)(2,1)} %feat_hbm.1), custom_call_target="tpu_custom_call" | custom-call | tf_op jit(solution)/shard_map/pallas_call | solution.py:452
  123.4 2.3 %copy.8 = bf16[1,1,128,4096]{3,2,1,0:T(8,128)(2,1)} copy(bf16[1,1,128,4096]{3,2,1,0:T(8,128)(2,1)} %shard_map.64) | data formatting | bytes 2097152

commit v3 on v2

--- a/solution.py
+++ b/solution.py
@@ -1,8 +1,8 @@
 import functools
-import random
 
 import jax
 import jax.numpy as jnp
+import numpy as np
 from jax import lax
 from jax.experimental import pallas as pl
 from jax.experimental.pallas import tpu as pltpu
@@ -18,67 +18,65 @@
 CHUNKS = 2 * NV + NC
 LINKS = 5
 LAG = 2
-PACE, GAP = 1, 1
+PACE = 1.0
 SLOTS = 4
 NONE = 4095
-ROUTE = (0.8, 4, 0.3, 3600, 2, 2)
+DUE = [
+    [[0.0, 0.5], [0.5849288578929801, 0.75], [0.9381583654646382, 1.42876989990142], [1.5, 1.75], [2.049650217767926, 2.430761940989174], [2.640286836685923, 2.90658948692369], [3.08954911142396, 3.24213595349004], [3.519824885989489, 3.7162593094967464]],
+    [[0.0, 0.5], [0.6767230009741291, 0.75], [1.0, 1.2668995343135907], [1.6244882778609058, 1.75], [2.1772854270325794, 2.430761940989174], [2.640286836685923, 3.0], [3.411816899315357, 3.545577257021955], [3.7467714995306727, 3.6597220473041556]],
+]
+ROUTE = (1.125, 0.007674667287227956, 0.4193835330241189, 0.25, 6075, DUE)
 
 
 def chunk_groups():
-    first = list(range(NV)) + list(range(2 * NV, CHUNKS))
-    return first, list(range(NV, NV + NV // 2)), list(range(NV + NV // 2, 2 * NV))
-
-
-def plan_routes(order_weight, rare_weight, noise, seed, late, last):
-    rnd = random.Random(seed)
+    return list(range(NV)) + list(range(2 * NV, CHUNKS)), list(range(NV, 2 * NV))
+
+
+def plan_routes(rare, rarer, reach_weight, noise, seed, due):
+    draw = np.random.RandomState(seed)
     nodes = [(x, z, q) for x in range(NX) for z in range(NZ) for q in range(NQ)]
     index = {n: i for i, n in enumerate(nodes)}
-    count = len(nodes)
-    goes = []
-    for x, z, q in nodes:
-        goes.append([
-            index[((x + 1) % NX, z, q)], index[((x - 1) % NX, z, q)],
-            index[(x, (z + 1) % NZ, q)], index[(x, (z - 1) % NZ, q)], index[(x, z, 1 - q)],
-        ])
-    _, second, third = chunk_groups()
-    due = []
-    for c in range(LAYERS * CHUNKS):
-        layer, part = divmod(c, CHUNKS)
-        steps = 2 * layer + (late if part in second + third else 0)
-        if layer == LAYERS - 1 and part in third:
-            steps += last
-        due.append(steps * order_weight / 2)
-    held = [{} for _ in nodes]
-    copies = [0] * (LAYERS * CHUNKS)
+    count, items, never = len(nodes), LAYERS * CHUNKS, 999
+    goes = np.array([
+        [index[((x + 1) % NX, z, q)], index[((x - 1) % NX, z, q)],
+         index[(x, (z + 1) % NZ, q)], index[(x, (z - 1) % NZ, q)], index[(x, z, 1 - q)]]
+        for x, z, q in nodes
+    ])
+    layer, part = np.arange(items) // CHUNKS, np.arange(items) % CHUNKS
+    group = ((part >= NV) & (part < 2 * NV)).astype(int)
+    slab = np.array([z // NK for _, z, _ in nodes])
+    when = np.full((count, items), never)
     for u, (x, z, q) in enumerate(nodes):
-        layer = z // NK * NX + x
-        for c in range(CHUNKS):
-            held[u][layer * CHUNKS + c] = 0
-            copies[layer * CHUNKS + c] += 1
-    missing = count * LAYERS * CHUNKS - sum(len(h) for h in held)
-    sends, ready = [], [0] * (LAYERS * CHUNKS)
-    while missing:
+        when[u, layer == z // NK * NX + x] = 0
+    urgency = np.array(due)[:, layer, group]
+    sends = []
+    while (when == never).any():
         r = len(sends)
+        reached, far = when < never, np.zeros(items)
+        copies = reached.sum(0) / count
+        for _ in range(8):
+            if reached.all():
+                break
+            far += ~reached.all(0)
+            wider = reached.copy()
+            for o in range(LINKS):
+                wider[goes[:, o]] |= reached
+            reached = wider
+        keys = (urgency + copies * (rare + rarer * r) - far * reach_weight)[slab]
+        jitter = draw.random_sample((count * LINKS, items)) * noise
+        held, free = when <= r, when == never
         row = [[NONE] * LINKS for _ in nodes]
-        turns = [(u, o) for u in range(count) for o in range(LINKS)]
-        rnd.shuffle(turns)
-        base = [due[c] + copies[c] / count * rare_weight for c in range(LAYERS * CHUNKS)]
-        for u, o in turns:
-            there = held[goes[u][o]]
-            best, best_key = None, None
-            for c, when in held[u].items():
-                if when <= r and c not in there:
-                    key = base[c] + rnd.random() * noise
-                    if best_key is None or key < best_key:
-                        best, best_key = c, key
-            if best is not None:
-                there[best] = r + LAG
-                copies[best] += 1
-                missing -= 1
-                ready[best] = max(ready[best], r + LAG)
+        for i in draw.permutation(count * LINKS):
+            u, o = divmod(int(i), LINKS)
+            v = goes[u, o]
+            key = np.where(held[u] & free[v], keys[v] + jitter[i], 1e9)
+            best = int(key.argmin())
+            if key[best] < 1e8:
+                free[v, best] = False
+                when[v, best] = r + LAG
                 row[u][o] = best % CHUNKS * LAYERS + best // CHUNKS
         sends.append(row)
-    return nodes, goes, sends, ready
+    return nodes, goes, sends, [int(t) for t in when.max(0)]
 
 
 def route_tables():
@@ -99,27 +97,22 @@
     def last_of(layer, group):
         return max(ready[layer * CHUNKS + c] for c in group)
 
-    first, second, third = chunk_groups()
-    pace, gap = PACE, GAP
-    starts, at = [], -pace
-    for layer in range(LAYERS):
-        need = last_of(layer, first) + gap
+    first, second = chunk_groups()
+    starts, at = [], -1
+    for layer in range(LAYERS + 1):
+        need = last_of(layer, first) if layer < LAYERS else 0
         if layer:
-            need = max(need, last_of(layer - 1, second + third) + gap)
-        at = max(at + pace, need)
-        starts.append(at)
-        at += pace
-        starts.append(at)
-    starts += [at + pace, at + 2 * pace]
-    at = max(at + 2 * pace + 1, last_of(LAYERS - 1, second) + gap)
-    starts.append(at)
-    starts.append(max(at + 1, last_of(LAYERS - 1, third) + gap))
+            need = max(need, last_of(layer - 1, second))
+        at = max(at + PACE, need)
+        starts.append(int(at))
+        at += PACE
+        starts.append(int(at))
     return starts
 
 
 def kernel(
     tables, v_hbm, u_hbm, c_hbm, gate_ref, bias_ref, feat_hbm, out_hbm,
-    W, E, X0, XC, ACC, DACC, BL, PS, PR, DS, DR, T_OUT, T_IN,
+    W, E, X0, XC, ACC, DACC, PS, PR, DS, DR, T_OUT, T_IN,
     local_sem, w_recv, e_recv, wd_recv, ed_recv, w_send, e_send, wd_send, ed_send,
     x_sem, p_send, p_recv, d_send, d_recv, o_local, o_send, o_recv,
 ):
@@ -264,33 +257,34 @@
 
     def traffic(r):
         slot0 = r % SLOTS * LINKS
-
-        @pl.when(r >= SLOTS)
-        def _():
-            for o in range(LINKS):
-                settle(w_send, e_send, slot0 + o, T_OUT[(r - SLOTS) * LINKS + o])
-                settle(wd_send, ed_send, slot0 + o, T_IN[(r - SLOTS) * LINKS + o])
-
+        came = [T_IN[r * LINKS + o] for o in range(LINKS)]
         for o in range(LINKS):
-            ident = T_IN[r * LINKS + o]
-
-            @pl.when(ident != NONE)
-            def _():
-                j, l = ident // LAYERS, ident % LAYERS
+            @pl.when(came[o] != NONE)
+            def _():
+                j, l = came[o] // LAYERS, came[o] % LAYERS
                 arrived(W.at[core, j, l], w_recv.at[j, l])
 
                 @pl.when(j == 2 * NV)
                 def _():
                     arrived(E.at[core, l], e_recv.at[l])
 
-                push(ident, slot0 + o, wd_send, ed_send, wd_recv, ed_recv, sibling)
-
         for o in range(LINKS):
-            ident_out = T_OUT[r * LINKS + o]
-
-            @pl.when(ident_out != NONE)
-            def _():
-                push(ident_out, slot0 + o, w_send, e_send, w_recv, e_recv, targets[o])
+            goes_out = T_OUT[r * LINKS + o]
+
+            @pl.when(goes_out != NONE)
+            def _():
+                push(goes_out, slot0 + o, w_send, e_send, w_recv, e_recv, targets[o])
+
+        for o in range(LINKS):
+            @pl.when(came[o] != NONE)
+            def _():
+                push(came[o], slot0 + o, wd_send, ed_send, wd_recv, ed_recv, sibling)
+
+    def settle_round(r):
+        for o in range(LINKS):
+            slot = r % SLOTS * LINKS + o
+            settle(w_send, e_send, slot, T_OUT[r * LINKS + o])
+            settle(wd_send, ed_send, slot, T_IN[r * LINKS + o])
 
     def weights_here(l, low, high, extra=False):
         @pl.when(l != sec)
@@ -336,30 +330,36 @@
             parts.append((gate * jnp.tanh(second)).astype(jnp.bfloat16))
         return jnp.concatenate(parts, axis=1)
 
-    def expand(blended, l, s, sub, b):
-        u_mat = W[sub, pl.ds(NV + deep * b, deep), l].reshape(piece, piece)
-        cross = jnp.dot(blended, u_mat, preferred_element_type=jnp.float32)
-        cols = pl.ds(pl.multiple_of(sub * sub_cols + b * piece, piece), piece)
-        new = XC[s, :, cols].astype(jnp.float32) + X0[s, :, cols].astype(jnp.float32) * (
-            cross + E[sub, l, pl.ds(b, 1), :])
-        XC[s, :, cols] = new.astype(jnp.bfloat16)
+    def results(b, s, sub):
+        at = sub * sub_cols + b * piece
+        src = slice(at, at + piece)
+        dst = out_hbm.at[0, 0, pl.ds(pl.multiple_of(s * block, block), block), pl.ds(pl.multiple_of(base + at, piece), piece)]
+        slot = b * 4 + s * 2 + sub
+        return remote(
+            XC.at[s, pl.ds(pl.multiple_of((1 - mine) * block, block), block), src], dst,
+            o_send.at[slot], o_recv.at[slot], pair)
+
+    def keep(b, s, sub):
+        at = sub * sub_cols + b * piece
+        own_rows = XC[s, pl.ds(pl.multiple_of(mine * block, block), block), at:at + piece]
+        out_hbm[0, 0, pl.ds(pl.multiple_of(s * block, block), block), pl.ds(pl.multiple_of(base + at, piece), piece)] = own_rows
 
     def finish(l, s):
         blended = blend(l, s)
-        for sub in range(2):
-            for b in range(2):
-                expand(blended, l, s, sub, b)
-
-    def results(b, s, sub):
-        at = sub * sub_cols + b * piece
-        src = pl.ds(pl.multiple_of(at, piece), piece)
-        dst = out_hbm.at[0, 0, s * block:(s + 1) * block, pl.ds(pl.multiple_of(base + at, piece), piece)]
-        slot = b * 4 + s * 2 + sub
-        return (
-            local(XC.at[s, pl.ds(pl.multiple_of(mine * block, block), block), src], dst, o_local.at[slot]),
-            remote(XC.at[s, pl.ds(pl.multiple_of((1 - mine) * block, block), block), src], dst,
-                   o_send.at[slot], o_recv.at[slot], pair),
-        )
+        for b in range(2):
+            for sub in range(2):
+                u_mat = W[sub, NV + deep * b:NV + deep * (b + 1), l].reshape(piece, piece)
+                cross = jnp.dot(blended, u_mat, preferred_element_type=jnp.float32)
+                at = sub * sub_cols + b * piece
+                cols = slice(at, at + piece)
+                new = XC[s, :, cols].astype(jnp.float32) + X0[s, :, cols].astype(jnp.float32) * (
+                    cross + E[sub, l, b:b + 1, :])
+                XC[s, :, cols] = new.astype(jnp.bfloat16)
+
+                @pl.when(l == LAYERS - 1)
+                def _():
+                    results(b, s, sub).start()
+                    keep(b, s, sub)
 
     def one_round(r, carry):
         @pl.when(r < rounds)
@@ -372,7 +372,7 @@
             step = step + jnp.where(r >= start, 1, 0)
             fires = fires + jnp.where(r == start, 1, 0)
 
-        @pl.when((fires > 0) & (step < 2 * LAYERS))
+        @pl.when(fires > 0)
         def _():
             l, s = step // 2, step % 2
 
@@ -392,36 +392,27 @@
                     weights_here(l - 1, NV, 2 * NV)
                 finish(l - 1, s)
 
-            @pl.when(s == 0)
-            def _():
-                weights_here(l, 0, NV)
-                weights_here(l, 2 * NV, CHUNKS, True)
-            project(l, s)
-
-        @pl.when((fires > 0) & (step >= 2 * LAYERS) & (step < 2 * LAYERS + 2))
-        def _():
-            BL[step % 2] = blend(LAYERS - 1, step % 2)
-
-        @pl.when((fires > 0) & (step >= 2 * LAYERS + 2))
-        def _():
-            b = step % 2
-            low = NV + b * (NV // 2)
-            weights_here(LAYERS - 1, low, low + NV // 2)
-            for s in range(2):
-                for sub in range(2):
-                    expand(BL[s], LAYERS - 1, s, sub, b)
-                    for copy in results(b, s, sub):
-                        copy.start()
+            @pl.when(l < LAYERS)
+            def _():
+                @pl.when(s == 0)
+                def _():
+                    weights_here(l, 0, NV)
+                    weights_here(l, 2 * NV, CHUNKS, True)
+                project(l, s)
+
+        @pl.when((r >= SLOTS - 1) & (r < rounds))
+        def _():
+            settle_round(r - (SLOTS - 1))
 
         return carry
 
     lax.fori_loop(0, total, one_round, 0)
 
-    for r in range(max(rounds - SLOTS, 0), rounds):
-        for o in range(LINKS):
-            slot = r % SLOTS * LINKS + o
-            settle(w_send, e_send, slot, T_OUT[r * LINKS + o])
-            settle(wd_send, ed_send, slot, T_IN[r * LINKS + o])
+    def last_rounds(r, carry):
+        settle_round(r)
+        return carry
+
+    lax.fori_loop(rounds - (SLOTS - 1), rounds, last_rounds, 0)
 
     def sent(i, carry):
         l, s = i // 2, i % 2
@@ -433,9 +424,7 @@
     for b in range(2):
         for s in range(2):
             for sub in range(2):
-                here, there = results(b, s, sub)
-                here.wait()
-                there.wait_send()
+                results(b, jnp.int32(s), sub).wait_send()
                 at = sub * sub_cols + b * piece
                 arrived(out_hbm.at[0, 0, s * block:(s + 1) * block, pl.ds(pl.multiple_of(other + at, piece), piece)],
                         o_recv.at[b * 4 + s * 2 + sub])
@@ -451,9 +440,9 @@
     dma = pltpu.SemaphoreType.DMA
     return pl.pallas_call(
         functools.partial(kernel, tables),
-        out_shape=jax.ShapeDtypeStruct(features.shape, features.dtype),
+        out_shape=pltpu.VMEM(features.shape, features.dtype),
         in_specs=[any_space] * 3 + [pl.BlockSpec(memory_space=pltpu.VMEM)] * 2 + [any_space],
-        out_specs=any_space,
+        out_specs=pl.BlockSpec(memory_space=pltpu.VMEM),
         scratch_shapes=[
             pltpu.VMEM((2, CHUNKS, LAYERS, PART, piece), jnp.bfloat16),
             pltpu.VMEM((2, LAYERS, 8, piece), jnp.float32),
@@ -461,7 +450,6 @@
             pltpu.VMEM((2, rows, half), jnp.bfloat16),
             pltpu.VMEM((2, rows, piece), jnp.float32),
             pltpu.VMEM((2, rows, 128), jnp.float32),
-            pltpu.VMEM((2, rows, piece), jnp.bfloat16),
             pltpu.VMEM((LAYERS, 2, rows, piece), jnp.bfloat16),
             pltpu.VMEM((LAYERS, 2, rows, piece), jnp.bfloat16),
             pltpu.VMEM((LAYERS, 2, 8, rows), jnp.float32),

time: 126 us -> 123 us (0.976)
  local copies, waits for them, and re-layouts: 2.29 us -> 0.97 us
    pallas_call x1, Pallas kernels: 123 us -> 122 us  [per_device(): pl.pallas_call(functools.partial(kernel, tables), out_shape=pltpu.VMEM(fe...]
    unnamed x1, local copies, waits for them, and re-layouts: 2.29 us -> 0.97 us
where the time goes in v3:
time: 123 us
  Pallas kernels  122 us (99%)
    pallas_call x1, Pallas kernels, per_device(): pl.pallas_call(functools.partial(kernel, tables), out_shape=pltpu.VMEM(fe...  122 us

profile of v3, /device:TPU:8, one launch (start us, length us, event | category | flops | bytes accessed | tf_op | source)
XLA Modules:
  0.0 122.9 jit_solution(3157712543889998059)
XLA Ops:
  0.0 122.0 %shard_map.64 = bf16[1,1,128,4096]{3,2,1,0:T(8,128)(2,1)S(1)} custom-call(bf16[1,4096,512]{2,1,0:T(8,128)(2,1)} %v_hbm.1, bf16[1,512,4096]{2,1,0:T(8,128)(2,1)} %u_hbm.1, bf16[1,2,256,256]{3,2,1,0:T(8,128)(2,1)} %c_hbm.1, bf16[1,2,4096]{2,1,0:T(2,128)(2,1)} %gate_ref.1, f32[1,4096]{1,0:T(1,128)} %bias_ref.1, bf16[1,1,128,4096]{3,2,1,0:T(8,128)(2,1)} %feat_hbm.1), custom_call_target="tpu_custom_call" | custom-call | tf_op jit(solution)/shard_map/pallas_call | solution.py:441
  122.0 1.0 copy.8

commit v4 on v3

--- a/solution.py
+++ b/solution.py
@@ -22,10 +22,10 @@
 SLOTS = 4
 NONE = 4095
 DUE = [
-    [[0.0, 0.5], [0.5849288578929801, 0.75], [0.9381583654646382, 1.42876989990142], [1.5, 1.75], [2.049650217767926, 2.430761940989174], [2.640286836685923, 2.90658948692369], [3.08954911142396, 3.24213595349004], [3.519824885989489, 3.7162593094967464]],
-    [[0.0, 0.5], [0.6767230009741291, 0.75], [1.0, 1.2668995343135907], [1.6244882778609058, 1.75], [2.1772854270325794, 2.430761940989174], [2.640286836685923, 3.0], [3.411816899315357, 3.545577257021955], [3.7467714995306727, 3.6597220473041556]],
+    [[0.0, 0.5], [0.5849288578929801, 1.2859887393727676], [0.9381583654646382, 1.1455558452467394], [1.3719483597663404, 1.6804870085712993], [2.049650217767926, 2.430761940989174], [2.640286836685923, 2.621520203407922], [3.08954911142396, 3.24213595349004], [3.303594641293013, 4.2123413743513884]],
+    [[0.0, 0.7683993199339043], [0.6767230009741291, 0.75], [1.0, 1.0688809251609854], [1.3719483597663404, 1.7424364088176243], [1.931100771933383, 2.516083922725886], [2.7223144702913498, 2.621520203407922], [3.411816899315357, 3.545577257021955], [3.7238975877989575, 4.430260712247482]],
 ]
-ROUTE = (1.125, 0.007674667287227956, 0.4193835330241189, 0.25, 6075, DUE)
+ROUTE = (1.125, 0.007674667287227956, 0.26778480630314494, 0.25, 6834, DUE)
 
 
 def chunk_groups():

time: 123 us -> 123 us (level)
  no operation moved by 1% of the time
where the time goes in v4:
time: 123 us; the launch traced here: 122 us
  Pallas kernels  121 us (98%)
    pallas_call x1, Pallas kernels, per_device(): pl.pallas_call(functools.partial(kernel, tables), out_shape=pltpu.VMEM(fe...  121 us

profile of v4, /device:TPU:8, one launch (start us, length us, event | category | flops | bytes accessed | tf_op | source)
XLA Modules:
  0.0 121.7 jit_solution(11843824641001057233)
XLA Ops:
  0.0 120.8 %shard_map.64 = bf16[1,1,128,4096]{3,2,1,0:T(8,128)(2,1)S(1)} custom-call(bf16[1,4096,512]{2,1,0:T(8,128)(2,1)} %v_hbm.1, bf16[1,512,4096]{2,1,0:T(8,128)(2,1)} %u_hbm.1, bf16[1,2,256,256]{3,2,1,0:T(8,128)(2,1)} %c_hbm.1, bf16[1,2,4096]{2,1,0:T(2,128)(2,1)} %gate_ref.1, f32[1,4096]{1,0:T(1,128)} %bias_ref.1, bf16[1,1,128,4096]{3,2,1,0:T(8,128)(2,1)} %feat_hbm.1), custom_call_target="tpu_custom_call" | custom-call | tf_op jit(solution)/shard_map/pallas_call | solution.py:441
  120.8 1.0 copy.8
